TPU v7x, 32 devices: a whole 2x2x4 slice. The times are simulated.
32 devices in a mesh: ctx: 8 (over y, x, core), tp: 4 (over z).
Axes of the slice: x: 2, y: 2, z: 4, core: 2. Of those that a mesh axis runs over, the one named last changes fastest.
Arguments:
- hidden_in: bfloat16 [2048, 4096], P(('ctx', 'tp')), may hold values from -6 to 6
- norm_gain: float32 [4096], replicated, may hold values from 0.5 to 1.5
- proj_weight: bfloat16 [4096, 4096], P(None, 'tp'), may hold values from -0.09375 to 0.09375
- conv_in: bfloat16 [2048, 4096], P('ctx', 'tp'), may hold values from -6 to 6
- conv_weight: float32 [4, 4096], P(None, 'tp'), may hold values from -3 to 3
- conv_bias: float32 [4096], P('tp'), may hold values from -3 to 3
- act_grad: bfloat16 [2048, 4096], P('ctx', 'tp'), may hold values from -6 to 6
Outputs:
- hidden_input_gradient: bfloat16 [2048, 4096], P(('ctx', 'tp'))
- norm_gain_gradient: float32 [4096], replicated
- taps_grad: float32 [4, 4096], P(None, 'tp')
- bias_grad: float32 [4096], P('tp')
All inputs are finite; a program needn't handle non-finite values.
Results may differ from a plain program's by a relative error of at most 0.013.
Values may be sent and summed in bfloat16 or wider, within the bound.
No kernel may reach another device: no remote copies, remote signals or barrier semaphores. Data moves between devices by JAX's collectives and lax.ppermute only.
A program may use at most 64 MiB of HBM per device.

v0:
```python
import jax
import jax.numpy as jnp
from jax import lax
from jax.sharding import PartitionSpec as P


def from_behind(block, axis, distance):
    devices = range(lax.axis_size(axis))
    route = [(i - distance, i) for i in devices if i - distance in devices]
    return lax.ppermute(block, axis, route)


def preact_of(padded, taps, offset, count_tok):
    tap_count = taps.shape[0]
    return offset[None, :] + sum(
        (
            taps[index][None, :] * padded[tap_count - 1 - index : tap_count - 1 - index + count_tok]
            for index in range(tap_count)
        )
    )


def grad_of(preact, cotangent):
    sigmoid_v = jax.nn.sigmoid(preact)
    return cotangent.astype(jnp.float32) * sigmoid_v * (1.0 + preact * (1.0 - sigmoid_v))


def on_device(hidden_in, norm_gain, proj_weight, conv_in, conv_weight, conv_bias, act_grad):
    count_tok = conv_in.shape[0]
    tap_count = conv_weight.shape[0]
    edge_rows = tap_count - 1
    earlier = from_behind(conv_in[count_tok - edge_rows :], "ctx", 1)
    later_in, later_grad = from_behind((conv_in[:edge_rows], act_grad[:edge_rows]), "ctx", -1)
    padded = jnp.concatenate([earlier, conv_in], 0).astype(jnp.float32)
    preact = preact_of(padded, conv_weight, conv_bias, count_tok)
    pre_grad = grad_of(preact, act_grad)
    tail_pad = jnp.concatenate([conv_in[count_tok - edge_rows :], later_in], 0).astype(jnp.float32)
    tail_pre = preact_of(tail_pad, conv_weight, conv_bias, edge_rows)
    next_grad = grad_of(tail_pre, later_grad)
    taps_part = jnp.stack(
        [
            jnp.sum(pre_grad * padded[edge_rows - index : edge_rows - index + count_tok], 0)
            for index in range(tap_count)
        ],
        0,
    )
    bias_part = jnp.sum(pre_grad, 0)
    taps_grad, bias_grad = lax.psum((taps_part, bias_part), "ctx")
    after = jnp.concatenate([pre_grad, next_grad], 0)
    in_grad = sum(
        (
            conv_weight[index][None, :] * after[index : index + count_tok]
            for index in range(tap_count)
        )
    ).astype(jnp.bfloat16)
    whole_term = lax.dot_general(
        in_grad, proj_weight, (((1,), (1,)), ((), ())), preferred_element_type=jnp.float32
    )
    normalized_gradient = lax.psum_scatter(
        whole_term.astype(jnp.bfloat16), "tp", scatter_dimension=0, tiled=True
    ).astype(jnp.float32)
    hidden_state = hidden_in.astype(jnp.float32)
    root_mean_square = jnp.sqrt(jnp.mean(hidden_state * hidden_state, -1, keepdims=True) + 1e-05)
    normalized_input = hidden_state / root_mean_square
    norm_gain_gradient = lax.psum(jnp.sum(normalized_gradient * normalized_input, 0), ("ctx", "tp"))
    scaled_gradient = norm_gain[None, :] * normalized_gradient
    mean_correction = jnp.mean(scaled_gradient * normalized_input, -1, keepdims=True)
    hidden_input_gradient = (
        (scaled_gradient - normalized_input * mean_correction) / root_mean_square
    ).astype(jnp.bfloat16)
    return (hidden_input_gradient, norm_gain_gradient, taps_grad, bias_grad)


def solution(mesh):
    return jax.shard_map(
        on_device,
        mesh=mesh,
        in_specs=(
            P(("ctx", "tp"), None),
            P(),
            P(None, "tp"),
            P("ctx", "tp"),
            P(None, "tp"),
            P("tp"),
            P("ctx", "tp"),
        ),
        out_specs=(P(("ctx", "tp"), None), P(), P(None, "tp"), P("tp")),
        check_vma=False,
    )
```

profile of v0, /device:TPU:0, one launch (start us, length us, event | category | flops | bytes accessed | tf_op | source)
XLA Modules:
  0.0 122.8 jit_solution(8762573390390648197)
XLA Ops:
  7.2 0.0 copy-start.2
  7.2 0.0 copy-start.4
  7.2 0.0 reduce-scatter.2.cloned.1.call-start
  7.2 0.8 fusion.26
  8.0 2.4 %collective-permute-start = (bf16[3,1024]{1,0:T(4,128)(2,1)S(1)}, bf16[3,1024]{1,0:T(4,128)(2,1)S(1)}, u32[]{:S(2)}, u32[]{:S(2)}) collective-permute-start(bf16[3,1024]{1,0:T(4,128)(2,1)S(1)} %get-tuple-element.14), channel_id=1, source_target_pairs={{0,4},{4,8},{8,12},{12,16},{16,20},{20,24},{24,28},{1,5},{5,9},{9,... | collective-permute-start | bytes 18440 | tf_op jit(solution)/shard_map/ppermute | solution.py:10
  10.4 1.3 %collective-permute-start.2 = (bf16[3,1024]{1,0:T(4,128)(2,1)S(1)}, bf16[3,1024]{1,0:T(4,128)(2,1)S(1)}, u32[]{:S(2)}, u32[]{:S(2)}) collective-permute-start(bf16[3,1024]{1,0:T(4,128)(2,1)S(1)} %get-tuple-element.15), channel_id=1, source_target_pairs={{4,0},{8,4},{12,8},{16,12},{20,16},{24,20},{28,24},{5,1},{9,5},{13... | collective-permute-start | bytes 18440 | tf_op jit(solution)/shard_map/ppermute | solution.py:10
  11.7 0.7 slice.76
  12.5 1.3 %collective-permute-start.1 = (bf16[3,1024]{1,0:T(4,128)(2,1)S(1)}, bf16[3,1024]{1,0:T(4,128)(2,1)S(1)}, u32[]{:S(2)}, u32[]{:S(2)}) collective-permute-start(bf16[3,1024]{1,0:T(4,128)(2,1)S(1)} %slice.76), channel_id=1, source_target_pairs={{4,0},{8,4},{12,8},{16,12},{20,16},{24,20},{28,24},{5,1},{9,5},{13... | collective-permute-start | bytes 18440 | tf_op jit(solution)/shard_map/ppermute | solution.py:10
  13.7 0.9 fusion.27
  14.6 0.0 collective-permute-done
  14.6 1.2 maximum_convert_fusion
  15.9 1.3 %multiply_reduce_fusion.3 = (f32[1024]{0:T(1024)S(1)}, f32[1024]{0:T(1024)S(1)}, f32[1024]{0:T(1024)S(1)}, f32[1024]{0:T(1024)S(1)}, f32[1024]{0:T(1024)S(1)}, /*index=5*/f32[256,1024]{1,0:T(8,128)S(1)}) fusion(f32[259,1024]{1,0:T(8,128)S(1)} %maximum_convert_fusion, f32[1024]{0:T(1024)S(1)} %bitcast.15, f32[1024]{0:T(1024)S(1)} %bitcast.18, ...), kind=kLoop, calls=%fused_computation.27 | loop fusion | flops 6810624 | bytes 5808128 | tf_op jit(solution)/shard_map/reduce_sum | solution.py:42
  17.1 0.0 collective-permute-done.2
  17.2 1.1 collective-permute-done.1
  18.3 7.4 %convolution_convert_fusion = bf16[256,4096]{1,0:T(8,128)(2,1)} fusion(bf16[4096,1024]{1,0:T(8,128)(2,1)} %param.9, f32[3,1024]{1,0:T(4,128)S(1)} %add_multiply_fusion.1, f32[256,1024]{1,0:T(8,128)S(1)} %get-tuple-element.13, f32[1024]{0:T(1024)S(1)} %bitcast.17, f32[1024]{0:T(1024)S(1)} %bitcast.20, f32[1024]{0:T(1024)S(1)} %bitcast.14, f32[1024]{0:T(1024)S(1)} %bitcast.11), kind=kOutput, calls=%fused_computation | convolution fusion | flops 2151415808 | bytes 11563008 | tf_op jit(solution)/shard_map/dot_general | solution.py:56
  25.6 0.0 reduce-scatter.2.cloned.1.call-update
  25.7 1.0 copy-done
  26.7 0.2 fusion.6
  26.9 29.4 %all-reduce = (f32[4,1024]{1,0:T(4,128)}, f32[1024]{0:T(1024)}) all-reduce(f32[4,1024]{1,0:T(4,128)S(1)} %pad_maximum_fusion.1, f32[1024]{0:T(1024)S(1)} %get-tuple-element.10), channel_id=1, replica_groups=mesh['ctx'=8,'tp'=4] {'ctx'}, use_global_device_ids=true, to_apply=%region_9.0 | all-reduce | flops 5120 | bytes 40960 | tf_op jit(solution)/shard_map/psum | solution.py:48
  56.4 17.4 %reduce-scatter.2.cloned.1.call-done = bf16[64,4096]{1,0:T(8,128)(2,1)} async-done(((bf16[256,4096]{1,0:T(8,128)(2,1)}), bf16[64,4096]{1,0:T(8,128)(2,1)}) %reduce-scatter.2.cloned.1.call-update) | async-done | bytes 524304 | tf_op jit(solution)/shard_map/reduce_scatter | solution.py:59
  73.7 1.6 %fusion.5 = (f32[4096]{0:T(1024)S(1)}, f32[64]{0:T(128)S(1)}) fusion(bf16[64,4096]{1,0:T(8,128)(2,1)} %reduce-scatter.2.cloned.1.call-done, f32[64]{0:T(128)S(1)} %add_sqrt_fusion, bf16[64,4096]{1,0:T(8,128)(2,1)S(1)} %copy-done, f32[4096]{0:T(1024)S(1)} %copy-done.3), kind=kLoop, calls=%fused_computation.12 | loop fusion | flops 2092992 | bytes 1081856 | tf_op jit(solution)/shard_map/reduce_sum | solution.py:65
  75.3 39.5 %psum.21 = f32[4096]{0:T(1024)} all-reduce(f32[4096]{0:T(1024)S(1)} %get-tuple-element.8), channel_id=1, replica_groups=mesh['ctx'=8,'tp'=4] {'ctx','tp'}, use_global_device_ids=true, to_apply=%region_4.0 | all-reduce | flops 4096 | bytes 32768 | tf_op jit(solution)/shard_map/psum | solution.py:65
  114.8 0.0 copy-done.1
  114.8 1.1 fusion.4
  (11 shorter events, 0.1 us)
Async XLA Ops:
  7.2 8.7 %copy-start.2 = (bf16[256,1024]{1,0:T(8,128)(2,1)S(1)}, bf16[256,1024]{1,0:T(8,128)(2,1)}, u32[]{:S(2)}) copy-start(bf16[256,1024]{1,0:T(8,128)(2,1)} %param.13) | copy-start | bytes 1572868
  7.2 8.7 %copy-start.4 = (f32[1024]{0:T(1024)S(1)}, f32[1024]{0:T(1024)}, u32[]{:S(2)}) copy-start(f32[1024]{0:T(1024)} %param.12) | copy-start | bytes 12292
  7.2 66.6 %reduce-scatter.2.cloned.1.call-start = ((), (), s32[]{:S(2)}) async-start(), calls=%async_computation.1 | async-start | bytes 2621440 | tf_op jit(solution)/shard_map/reduce_scatter | solution.py:59
  8.0 6.6 %collective-permute-start = (bf16[3,1024]{1,0:T(4,128)(2,1)S(1)}, bf16[3,1024]{1,0:T(4,128)(2,1)S(1)}, u32[]{:S(2)}, u32[]{:S(2)}) collective-permute-start(bf16[3,1024]{1,0:T(4,128)(2,1)S(1)} %get-tuple-element.14), channel_id=1, source_target_pairs={{0,4},{4,8},{8,12},{12,16},{16,20},{20,24},{24,28},{1,5},{5,9},{9,... | collective-permute-start | bytes 18440 | tf_op jit(solution)/shard_map/ppermute | solution.py:10
  10.4 6.7 %collective-permute-start.2 = (bf16[3,1024]{1,0:T(4,128)(2,1)S(1)}, bf16[3,1024]{1,0:T(4,128)(2,1)S(1)}, u32[]{:S(2)}, u32[]{:S(2)}) collective-permute-start(bf16[3,1024]{1,0:T(4,128)(2,1)S(1)} %get-tuple-element.15), channel_id=1, source_target_pairs={{4,0},{8,4},{12,8},{16,12},{20,16},{24,20},{28,24},{5,1},{9,5},{13... | collective-permute-start | bytes 18440 | tf_op jit(solution)/shard_map/ppermute | solution.py:10
  12.5 5.8 %collective-permute-start.1 = (bf16[3,1024]{1,0:T(4,128)(2,1)S(1)}, bf16[3,1024]{1,0:T(4,128)(2,1)S(1)}, u32[]{:S(2)}, u32[]{:S(2)}) collective-permute-start(bf16[3,1024]{1,0:T(4,128)(2,1)S(1)} %slice.76), channel_id=1, source_target_pairs={{4,0},{8,4},{12,8},{16,12},{20,16},{24,20},{28,24},{5,1},{9,5},{13... | collective-permute-start | bytes 18440 | tf_op jit(solution)/shard_map/ppermute | solution.py:10
  25.6 1.0 copy-start
  25.6 48.1 %copy-start.3 = (f32[4096]{0:T(1024)S(1)}, f32[4096]{0:T(1024)}, u32[]{:S(2)}) copy-start(f32[4096]{0:T(1024)} %param.8) | copy-start | bytes 49156
  73.7 41.1 %copy-start.1 = (bf16[64,4096]{1,0:T(8,128)(2,1)S(1)}, bf16[64,4096]{1,0:T(8,128)(2,1)}, u32[]{:S(2)}) copy-start(bf16[64,4096]{1,0:T(8,128)(2,1)} %reduce-scatter.2.cloned.1.call-done) | copy-start | bytes 1572868
Sparse Core Ops, SparseCore 0:
  25.8 47.9 reduce-scatter.1
where the time goes:
time: 123 us
  blocking collectives  68.9 us (56%)
  waiting for transfers between devices  18.5 us (15%)
  between operations  14.1 us (11%)
  matrix products  7.36 us (6%)
  other arithmetic  5.41 us (4%)
  starting transfers between devices  5.01 us (4%)
  local copies, waits for them, and re-layouts  3.44 us (3%)
    psum x1, blocking collectives, on_device(): lax.psum(jnp.sum(normalized_gradient * normalized_input, 0), ('ctx', 'tp'))  39.5 us
    psum x1, blocking collectives, on_device(): taps_grad, bias_grad = lax.psum((taps_part, bias_part), 'ctx')  29.4 us
    reduce_scatter x1, waiting for transfers between devices, on_device(): lax.psum_scatter(whole_term.astype(jnp.bfloat16), 'tp', scatter_dimension...  17.4 us
    dot_general x1, matrix products, on_device(): lax.dot_general(in_grad, proj_weight, (((1,), (1,)), ((), ())), preferred...  7.36 us
    ppermute x3, starting transfers between devices, from_behind(): return lax.ppermute(block, axis, route)  4.97 us
  transfers between devices with their start and end apart: 4, of which 2 were waited for; matrix products, arithmetic and copies ran while one was open for 4% of the time, Pallas kernels for 0%

commit v1 on v0

--- a/solution.py
+++ b/solution.py
@@ -25,27 +25,60 @@
     return cotangent.astype(jnp.float32) * sigmoid_v * (1.0 + preact * (1.0 - sigmoid_v))
 
 
+def xor_sum(value, axis):
+    size = lax.axis_size(axis)
+    if size & (size - 1):
+        return lax.psum(value, axis)
+    step = 1
+    while step < size:
+        value = value + lax.ppermute(value, axis, [(i, i ^ step) for i in range(size)])
+        step *= 2
+    return value
+
+
+def line_scatter_parts(part, axis):
+    size = lax.axis_size(axis)
+    place = lax.axis_index(axis)
+    rows = part.shape[0] // size
+
+    def block(index):
+        return lax.dynamic_slice_in_dim(part, jnp.clip(index, 0, size - 1) * rows, rows, 0)
+
+    def joined(own, arrived):
+        if arrived is None:
+            return own
+        return (own.astype(jnp.float32) + arrived.astype(jnp.float32)).astype(part.dtype)
+
+    right = left = None
+    for hop in range(1, size):
+        send_right = joined(block(size - hop + place), right)
+        send_left = joined(block(hop - size + place), left)
+        right = lax.ppermute(send_right, axis, [(i, i + 1) for i in range(hop)])
+        left = lax.ppermute(send_left, axis, [(size - 1 - i, size - 2 - i) for i in range(hop)])
+        if hop < size - 1:
+            yield None
+    total = block(place).astype(jnp.float32)
+    if right is not None:
+        total = total + right.astype(jnp.float32) + left.astype(jnp.float32)
+    yield total
+
+
+CHUNKS = 2
+
+
 def on_device(hidden_in, norm_gain, proj_weight, conv_in, conv_weight, conv_bias, act_grad):
     count_tok = conv_in.shape[0]
     tap_count = conv_weight.shape[0]
     edge_rows = tap_count - 1
     earlier = from_behind(conv_in[count_tok - edge_rows :], "ctx", 1)
-    later_in, later_grad = from_behind((conv_in[:edge_rows], act_grad[:edge_rows]), "ctx", -1)
+    later = from_behind(jnp.concatenate([conv_in[:edge_rows], act_grad[:edge_rows]], 0), "ctx", -1)
+    later_in, later_grad = later[:edge_rows], later[edge_rows:]
     padded = jnp.concatenate([earlier, conv_in], 0).astype(jnp.float32)
     preact = preact_of(padded, conv_weight, conv_bias, count_tok)
     pre_grad = grad_of(preact, act_grad)
     tail_pad = jnp.concatenate([conv_in[count_tok - edge_rows :], later_in], 0).astype(jnp.float32)
     tail_pre = preact_of(tail_pad, conv_weight, conv_bias, edge_rows)
     next_grad = grad_of(tail_pre, later_grad)
-    taps_part = jnp.stack(
-        [
-            jnp.sum(pre_grad * padded[edge_rows - index : edge_rows - index + count_tok], 0)
-            for index in range(tap_count)
-        ],
-        0,
-    )
-    bias_part = jnp.sum(pre_grad, 0)
-    taps_grad, bias_grad = lax.psum((taps_part, bias_part), "ctx")
     after = jnp.concatenate([pre_grad, next_grad], 0)
     in_grad = sum(
         (
@@ -53,16 +86,39 @@
             for index in range(tap_count)
         )
     ).astype(jnp.bfloat16)
-    whole_term = lax.dot_general(
-        in_grad, proj_weight, (((1,), (1,)), ((), ())), preferred_element_type=jnp.float32
+    in_grad = lax.optimization_barrier(in_grad)
+    width = proj_weight.shape[0]
+    chunk = width // CHUNKS
+    streams = []
+    for index in range(CHUNKS):
+        part = lax.dot_general(
+            in_grad,
+            proj_weight[index * chunk : (index + 1) * chunk],
+            (((1,), (1,)), ((), ())),
+            preferred_element_type=jnp.float32,
+        ).astype(jnp.bfloat16)
+        streams.append(line_scatter_parts(lax.optimization_barrier(part), "tp"))
+    sums = [None] * CHUNKS
+    for _ in range(max(lax.axis_size("tp") - 1, 1)):
+        for index in range(CHUNKS):
+            sums[index] = next(streams[index])
+    taps_part = jnp.stack(
+        [
+            jnp.sum(pre_grad * padded[edge_rows - index : edge_rows - index + count_tok], 0)
+            for index in range(tap_count)
+        ]
+        + [jnp.sum(pre_grad, 0)],
+        0,
     )
-    normalized_gradient = lax.psum_scatter(
-        whole_term.astype(jnp.bfloat16), "tp", scatter_dimension=0, tiled=True
-    ).astype(jnp.float32)
+    taps_all = xor_sum(taps_part, "ctx")
+    taps_grad, bias_grad = taps_all[:tap_count], taps_all[tap_count]
+    normalized_gradient = jnp.concatenate(sums, 1)
     hidden_state = hidden_in.astype(jnp.float32)
     root_mean_square = jnp.sqrt(jnp.mean(hidden_state * hidden_state, -1, keepdims=True) + 1e-05)
     normalized_input = hidden_state / root_mean_square
-    norm_gain_gradient = lax.psum(jnp.sum(normalized_gradient * normalized_input, 0), ("ctx", "tp"))
+    norm_gain_gradient = xor_sum(
+        xor_sum(jnp.sum(normalized_gradient * normalized_input, 0), "ctx"), "tp"
+    )
     scaled_gradient = norm_gain[None, :] * normalized_gradient
     mean_correction = jnp.mean(scaled_gradient * normalized_input, -1, keepdims=True)
     hidden_input_gradient = (

time: 123 us -> 87.2 us (0.71)
  blocking collectives: 68.9 us -> 0 us
  starting transfers between devices: 5.01 us -> 46.5 us
  between operations: 14.1 us -> 1.06 us
  waiting for transfers between devices: 18.5 us -> 21.1 us
  other arithmetic: 5.41 us -> 7.13 us
    psum x2 -> x0, blocking collectives: 68.9 us -> none  [the longest x1 39.5 us: on_device(): lax.psum(jnp.sum(normalized_gradient * normalized_input, 0), ('ctx', 'tp'))]
    ppermute x0 -> x20, starting transfers between devices: none -> 42.8 us  [the longest x6 23.5 us: line_scatter_parts(): right = lax.ppermute(send_right, axis, [(i, i + 1) for i in range(hop)])]
    ppermute x0 -> x20, waiting for transfers between devices: none -> 21 us  [the longest x6 11.2 us: line_scatter_parts(): lax.ppermute(send_left, axis, [(size - 1 - i, size - 2 - i) for i in rang...]
    reduce_scatter x1 -> x0, waiting for transfers between devices: 17.4 us -> none  [on_device(): lax.psum_scatter(whole_term.astype(jnp.bfloat16), 'tp', scatter_dimension...]
    ppermute x3 -> x2, starting transfers between devices: 4.97 us -> 3.69 us  [from_behind(): return lax.ppermute(block, axis, route)]
    dot_general x1 -> x2, matrix products: 7.36 us -> 6.95 us  [on_device(): lax.dot_general(in_grad, proj_weight[index * chunk:(index + 1) * chunk],...]
  transfers between devices with their start and end apart: 4 -> 22, of which waited for: 2 -> 9; matrix products, arithmetic and copies ran while one was open for 4% -> 19% of each run, Pallas kernels for 0% -> 0%
where the time goes in v1:
time: 87.2 us; the launch traced here: 86.5 us
  starting transfers between devices  46.5 us (53%)
  waiting for transfers between devices  21.1 us (24%)
  other arithmetic  7.13 us (8%)
  matrix products  6.95 us (8%)
  local copies, waits for them, and re-layouts  3.79 us (4%)
  between operations  1.06 us (1%)
    ppermute x6, starting transfers between devices, line_scatter_parts(): right = lax.ppermute(send_right, axis, [(i, i + 1) for i in range(hop)])  23.5 us
    ppermute x8, starting transfers between devices, xor_sum(): lax.ppermute(value, axis, [(i, i ^ step) for i in range(size)])  14 us
    ppermute x6, waiting for transfers between devices, line_scatter_parts(): lax.ppermute(send_left, axis, [(size - 1 - i, size - 2 - i) for i in rang...  11.2 us
    dot_general x2, matrix products, on_device(): lax.dot_general(in_grad, proj_weight[index * chunk:(index + 1) * chunk],...  6.95 us
    ppermute x8, waiting for transfers between devices, xor_sum(): lax.ppermute(value, axis, [(i, i ^ step) for i in range(size)])  6.74 us
    ppermute x6, starting transfers between devices, line_scatter_parts(): lax.ppermute(send_left, axis, [(size - 1 - i, size - 2 - i) for i in rang...  5.29 us
    ppermute x2, starting transfers between devices, from_behind(): return lax.ppermute(block, axis, route)  3.69 us
    ppermute x6, waiting for transfers between devices, line_scatter_parts(): right = lax.ppermute(send_right, axis, [(i, i + 1) for i in range(hop)])  3.06 us
  transfers between devices with their start and end apart: 22, of which 9 were waited for; matrix products, arithmetic and copies ran while one was open for 19% of the time, Pallas kernels for 0%

profile of v1, /device:TPU:0, one launch (start us, length us, event | category | flops | bytes accessed | tf_op | source)
XLA Modules:
  0.0 86.5 jit_solution(15161204780941501451)
XLA Ops:
  1.5 2.4 %collective-permute-start = (bf16[3,1024]{1,0:T(4,128)(2,1)S(1)}, bf16[3,1024]{1,0:T(4,128)(2,1)S(1)}, u32[]{:S(2)}, u32[]{:S(2)}) collective-permute-start(bf16[3,1024]{1,0:T(4,128)(2,1)S(1)} %get-tuple-element.20), channel_id=1, source_target_pairs={{0,4},{4,8},{8,12},{12,16},{16,20},{20,24},{24,28},{1,5},{5,9},{9,... | collective-permute-start | bytes 18440 | tf_op jit(solution)/shard_map/ppermute | solution.py:10
  4.6 1.3 %collective-permute-start.1 = (bf16[6,1024]{1,0:T(8,128)(2,1)S(1)}, bf16[6,1024]{1,0:T(8,128)(2,1)S(1)}, u32[]{:S(2)}, u32[]{:S(2)}) collective-permute-start(bf16[6,1024]{1,0:T(8,128)(2,1)S(1)} %pad_maximum_fusion.2), channel_id=1, source_target_pairs={{4,0},{8,4},{12,8},{16,12},{20,16},{24,20},{28,24},{5,1},{9,5},{13... | collective-permute-start | bytes 36872 | tf_op jit(solution)/shard_map/ppermute | solution.py:10
  6.8 1.2 %fusion.10 = f32[64]{0:T(128)S(1)} fusion(bf16[64,4096]{1,0:T(8,128)(2,1)} %param.7), kind=kLoop, calls=%fused_computation.10 | loop fusion | flops 786368 | bytes 524544 | tf_op jit(solution)/shard_map/reduce_sum | solution.py:117
  9.3 1.3 %multiply_reduce_fusion = (f32[1024]{0:T(1024)S(1)}, f32[1024]{0:T(1024)S(1)}, f32[1024]{0:T(1024)S(1)}, f32[1024]{0:T(1024)S(1)}, f32[1024]{0:T(1024)S(1)}, /*index=5*/f32[256,1024]{1,0:T(8,128)S(1)}) fusion(f32[259,1024]{1,0:T(8,128)S(1)} %maximum_convert_fusion, f32[1024]{0:T(1024)S(1)} %bitcast.18, f32[1024]{0:T(1024)S(1)} %bitcast.21, ...), kind=kLoop, calls=%fused_computation.22 | loop fusion | flops 6810624 | bytes 5808128 | tf_op jit(solution)/shard_map/reduce_sum | solution.py:107
  10.6 3.3 %collective-permute-start.19 = (f32[5,1024]{1,0:T(8,128)S(1)}, f32[5,1024]{1,0:T(8,128)S(1)}, u32[]{:S(2)}, u32[]{:S(2)}) collective-permute-start(f32[5,1024]{1,0:T(8,128)S(1)} %stack.23), channel_id=1, source_target_pairs={{0,4},{4,0},{8,12},{12,8},{16,20},{20,16},{24,28},{28,24},{1,5},{5... | collective-permute-start | bytes 61448 | tf_op jit(solution)/shard_map/ppermute | solution.py:34
  14.5 3.5 %fusion.4 = bf16[256,2048]{1,0:T(8,128)(2,1)S(1)} fusion(bf16[256,1024]{1,0:T(8,128)(2,1)S(1)} %fusion.15, bf16[4096,1024]{1,0:T(8,128)(2,1)} %param.9), kind=kOutput, calls=%fused_computation.4 | convolution fusion | flops 1074266112 | bytes 5767168 | tf_op jit(solution)/shard_map/dot_general | solution.py:94
  18.0 3.5 %collective-permute-start.2 = (bf16[64,2048]{1,0:T(8,128)(2,1)S(1)}, bf16[64,2048]{1,0:T(8,128)(2,1)S(1)}, u32[]{:S(2)}, u32[]{:S(2)}) collective-permute-start(bf16[64,2048]{1,0:T(8,128)(2,1)S(1)} %get-tuple-element.14), channel_id=1, source_target_pairs={{0,1},{4,5},{8,9},{12,13},{16,17},{20,21},{24,25},{28,29}} | collective-permute-start | bytes 786440 | tf_op jit(solution)/shard_map/ppermute | solution.py:56
  21.5 3.5 %fusion.7 = bf16[256,2048]{1,0:T(8,128)(2,1)S(1)} fusion(bf16[256,1024]{1,0:T(8,128)(2,1)S(1)} %fusion.15, bf16[4096,1024]{1,0:T(8,128)(2,1)} %param.9), kind=kOutput, calls=%fused_computation.5 | convolution fusion | flops 1074266112 | bytes 5767168 | tf_op jit(solution)/shard_map/dot_general | solution.py:94
  25.7 1.3 %collective-permute-start.8 = (bf16[64,2048]{1,0:T(8,128)(2,1)S(1)}, bf16[64,2048]{1,0:T(8,128)(2,1)S(1)}, u32[]{:S(2)}, u32[]{:S(2)}) collective-permute-start(bf16[64,2048]{1,0:T(8,128)(2,1)S(1)} %get-tuple-element.18), channel_id=1, source_target_pairs={{0,1},{4,5},{8,9},{12,13},{16,17},{20,21},{24,25},{28,29}} | collective-permute-start | bytes 786440 | tf_op jit(solution)/shard_map/ppermute | solution.py:56
  27.8 4.0 %collective-permute-start.3 = (bf16[64,2048]{1,0:T(8,128)(2,1)S(1)}, bf16[64,2048]{1,0:T(8,128)(2,1)S(1)}, u32[]{:S(2)}, u32[]{:S(2)}) collective-permute-start(bf16[64,2048]{1,0:T(8,128)(2,1)S(1)} %add_convert_fusion.7), channel_id=1, source_target_pairs={{0,1},{1,2},{4,5},{5,6},{8,9},{9,10},{12,13},{13,14},{16,17},{17,1... | collective-permute-start | bytes 786440 | tf_op jit(solution)/shard_map/ppermute | solution.py:56
  31.8 1.9 %collective-permute-done.8 = bf16[64,2048]{1,0:T(8,128)(2,1)S(1)} collective-permute-done((bf16[64,2048]{1,0:T(8,128)(2,1)S(1)}, bf16[64,2048]{1,0:T(8,128)(2,1)S(1)}, u32[]{:S(2)}, u32[]{:S(2)}) %collective-permute-start.8) | collective-permute-done | bytes 262176 | tf_op jit(solution)/shard_map/ppermute | solution.py:56
  33.8 4.4 %collective-permute-start.9 = (bf16[64,2048]{1,0:T(8,128)(2,1)S(1)}, bf16[64,2048]{1,0:T(8,128)(2,1)S(1)}, u32[]{:S(2)}, u32[]{:S(2)}) collective-permute-start(bf16[64,2048]{1,0:T(8,128)(2,1)S(1)} %add_convert_fusion.3), channel_id=1, source_target_pairs={{0,1},{1,2},{4,5},{5,6},{8,9},{9,10},{12,13},{13,14},{16,17},{17,1... | collective-permute-start | bytes 786440 | tf_op jit(solution)/shard_map/ppermute | solution.py:56
  40.1 5.0 %collective-permute-start.4 = (bf16[64,2048]{1,0:T(8,128)(2,1)S(1)}, bf16[64,2048]{1,0:T(8,128)(2,1)S(1)}, u32[]{:S(2)}, u32[]{:S(2)}) collective-permute-start(bf16[64,2048]{1,0:T(8,128)(2,1)S(1)} %get-tuple-element.12), channel_id=1, source_target_pairs={{0,1},{1,2},{2,3},{4,5},{5,6},{6,7},{8,9},{9,10},{10,11},{12,13},{... | collective-permute-start | bytes 786440 | tf_op jit(solution)/shard_map/ppermute | solution.py:56
  46.0 5.3 %collective-permute-start.10 = (bf16[64,2048]{1,0:T(8,128)(2,1)S(1)}, bf16[64,2048]{1,0:T(8,128)(2,1)S(1)}, u32[]{:S(2)}, u32[]{:S(2)}) collective-permute-start(bf16[64,2048]{1,0:T(8,128)(2,1)S(1)} %get-tuple-element.16), channel_id=1, source_target_pairs={{0,1},{1,2},{2,3},{4,5},{5,6},{6,7},{8,9},{9,10},{10,11},{12,13},{... | collective-permute-start | bytes 786440 | tf_op jit(solution)/shard_map/ppermute | solution.py:56
  51.4 1.3 %collective-permute-start.7 = (bf16[64,2048]{1,0:T(8,128)(2,1)S(1)}, bf16[64,2048]{1,0:T(8,128)(2,1)S(1)}, u32[]{:S(2)}, u32[]{:S(2)}) collective-permute-start(bf16[64,2048]{1,0:T(8,128)(2,1)S(1)} %add_convert_fusion.4), channel_id=1, source_target_pairs={{3,2},{2,1},{1,0},{7,6},{6,5},{5,4},{11,10},{10,9},{9,8},{15,14},{... | collective-permute-start | bytes 786440 | tf_op jit(solution)/shard_map/ppermute | solution.py:57
  52.8 1.3 %collective-permute-start.13 = (bf16[64,2048]{1,0:T(8,128)(2,1)S(1)}, bf16[64,2048]{1,0:T(8,128)(2,1)S(1)}, u32[]{:S(2)}, u32[]{:S(2)}) collective-permute-start(bf16[64,2048]{1,0:T(8,128)(2,1)S(1)} %add_convert_fusion), channel_id=1, source_target_pairs={{3,2},{2,1},{1,0},{7,6},{6,5},{5,4},{11,10},{10,9},{9,8},{15,14},{... | collective-permute-start | bytes 786440 | tf_op jit(solution)/shard_map/ppermute | solution.py:57
  54.1 8.5 %collective-permute-done.7 = bf16[64,2048]{1,0:T(8,128)(2,1)S(1)} collective-permute-done((bf16[64,2048]{1,0:T(8,128)(2,1)S(1)}, bf16[64,2048]{1,0:T(8,128)(2,1)S(1)}, u32[]{:S(2)}, u32[]{:S(2)}) %collective-permute-start.7) | collective-permute-done | bytes 262176 | tf_op jit(solution)/shard_map/ppermute | solution.py:57
  62.8 2.7 %collective-permute-done.13 = bf16[64,2048]{1,0:T(8,128)(2,1)S(1)} collective-permute-done((bf16[64,2048]{1,0:T(8,128)(2,1)S(1)}, bf16[64,2048]{1,0:T(8,128)(2,1)S(1)}, u32[]{:S(2)}, u32[]{:S(2)}) %collective-permute-start.13) | collective-permute-done | bytes 262176 | tf_op jit(solution)/shard_map/ppermute | solution.py:57
  66.1 2.6 %collective-permute-start.20 = (f32[5,1024]{1,0:T(8,128)S(1)}, f32[5,1024]{1,0:T(8,128)S(1)}, u32[]{:S(2)}, u32[]{:S(2)}) collective-permute-start(f32[5,1024]{1,0:T(8,128)S(1)} %add.227), channel_id=1, source_target_pairs={{0,8},{4,12},{8,0},{12,4},{16,24},{20,28},{24,16},{28,20},{1,9},{5... | collective-permute-start | bytes 61448 | tf_op jit(solution)/shard_map/ppermute | solution.py:34
  70.8 2.9 %collective-permute-start.21 = (f32[5,1024]{1,0:T(8,128)S(1)}, f32[5,1024]{1,0:T(8,128)S(1)}, u32[]{:S(2)}, u32[]{:S(2)}) collective-permute-start(f32[5,1024]{1,0:T(8,128)S(1)} %add.228), channel_id=1, source_target_pairs={{0,16},{4,20},{8,24},{12,28},{16,0},{20,4},{24,8},{28,12},{1,17},{... | collective-permute-start | bytes 61448 | tf_op jit(solution)/shard_map/ppermute | solution.py:34
  77.5 1.8 %collective-permute-start.17 = (f32[4096]{0:T(1024)S(1)}, f32[4096]{0:T(1024)S(1)}, u32[]{:S(2)}, u32[]{:S(2)}) collective-permute-start(f32[4096]{0:T(1024)S(1)} %add.224), channel_id=1, source_target_pairs={{0,1},{1,0},{2,3},{3,2},{4,5},{5,4},{6,7},{7,6},{8,9},{9,8},{10,11... | collective-permute-start | bytes 49160 | tf_op jit(solution)/shard_map/ppermute | solution.py:34
  79.3 1.9 %collective-permute-done.17 = f32[4096]{0:T(1024)S(1)} collective-permute-done((f32[4096]{0:T(1024)S(1)}, f32[4096]{0:T(1024)S(1)}, u32[]{:S(2)}, u32[]{:S(2)}) %collective-permute-start.17) | collective-permute-done | bytes 16416 | tf_op jit(solution)/shard_map/ppermute | solution.py:34
  81.2 1.5 %collective-permute-start.18 = (f32[4096]{0:T(1024)S(1)}, f32[4096]{0:T(1024)S(1)}, u32[]{:S(2)}, u32[]{:S(2)}) collective-permute-start(f32[4096]{0:T(1024)S(1)} %add.225), channel_id=1, source_target_pairs={{0,2},{1,3},{2,0},{3,1},{4,6},{5,7},{6,4},{7,5},{8,10},{9,11},{10,... | collective-permute-start | bytes 49160 | tf_op jit(solution)/shard_map/ppermute | solution.py:34
  83.8 2.1 %collective-permute-done.18 = f32[4096]{0:T(1024)S(1)} collective-permute-done((f32[4096]{0:T(1024)S(1)}, f32[4096]{0:T(1024)S(1)}, u32[]{:S(2)}, u32[]{:S(2)}) %collective-permute-start.18) | collective-permute-done | bytes 16416 | tf_op jit(solution)/shard_map/ppermute | solution.py:34
  (66 shorter events, 17.0 us)
Async XLA Ops:
  1.5 6.6 %collective-permute-start = (bf16[3,1024]{1,0:T(4,128)(2,1)S(1)}, bf16[3,1024]{1,0:T(4,128)(2,1)S(1)}, u32[]{:S(2)}, u32[]{:S(2)}) collective-permute-start(bf16[3,1024]{1,0:T(4,128)(2,1)S(1)} %get-tuple-element.20), channel_id=1, source_target_pairs={{0,4},{4,8},{8,12},{12,16},{16,20},{20,24},{24,28},{1,5},{5,9},{9,... | collective-permute-start | bytes 18440 | tf_op jit(solution)/shard_map/ppermute | solution.py:10
  4.6 9.3 %collective-permute-start.1 = (bf16[6,1024]{1,0:T(8,128)(2,1)S(1)}, bf16[6,1024]{1,0:T(8,128)(2,1)S(1)}, u32[]{:S(2)}, u32[]{:S(2)}) collective-permute-start(bf16[6,1024]{1,0:T(8,128)(2,1)S(1)} %pad_maximum_fusion.2), channel_id=1, source_target_pairs={{4,0},{8,4},{12,8},{16,12},{20,16},{24,20},{28,24},{5,1},{9,5},{13... | collective-permute-start | bytes 36872 | tf_op jit(solution)/shard_map/ppermute | solution.py:10
  10.6 55.5 %collective-permute-start.19 = (f32[5,1024]{1,0:T(8,128)S(1)}, f32[5,1024]{1,0:T(8,128)S(1)}, u32[]{:S(2)}, u32[]{:S(2)}) collective-permute-start(f32[5,1024]{1,0:T(8,128)S(1)} %stack.23), channel_id=1, source_target_pairs={{0,4},{4,0},{8,12},{12,8},{16,20},{20,16},{24,28},{28,24},{1,5},{5... | collective-permute-start | bytes 61448 | tf_op jit(solution)/shard_map/ppermute | solution.py:34
  18.0 9.7 %collective-permute-start.2 = (bf16[64,2048]{1,0:T(8,128)(2,1)S(1)}, bf16[64,2048]{1,0:T(8,128)(2,1)S(1)}, u32[]{:S(2)}, u32[]{:S(2)}) collective-permute-start(bf16[64,2048]{1,0:T(8,128)(2,1)S(1)} %get-tuple-element.14), channel_id=1, source_target_pairs={{0,1},{4,5},{8,9},{12,13},{16,17},{20,21},{24,25},{28,29}} | collective-permute-start | bytes 786440 | tf_op jit(solution)/shard_map/ppermute | solution.py:56
  25.0 13.2 %collective-permute-start.5 = (bf16[64,2048]{1,0:T(8,128)(2,1)S(1)}, bf16[64,2048]{1,0:T(8,128)(2,1)S(1)}, u32[]{:S(2)}, u32[]{:S(2)}) collective-permute-start(bf16[64,2048]{1,0:T(8,128)(2,1)S(1)} %get-tuple-element.15), channel_id=1, source_target_pairs={{3,2},{7,6},{11,10},{15,14},{19,18},{23,22},{27,26},{31,30}} | collective-permute-start | bytes 786440 | tf_op jit(solution)/shard_map/ppermute | solution.py:57
  25.7 8.0 %collective-permute-start.8 = (bf16[64,2048]{1,0:T(8,128)(2,1)S(1)}, bf16[64,2048]{1,0:T(8,128)(2,1)S(1)}, u32[]{:S(2)}, u32[]{:S(2)}) collective-permute-start(bf16[64,2048]{1,0:T(8,128)(2,1)S(1)} %get-tuple-element.18), channel_id=1, source_target_pairs={{0,1},{4,5},{8,9},{12,13},{16,17},{20,21},{24,25},{28,29}} | collective-permute-start | bytes 786440 | tf_op jit(solution)/shard_map/ppermute | solution.py:56
  27.0 18.1 %collective-permute-start.11 = (bf16[64,2048]{1,0:T(8,128)(2,1)S(1)}, bf16[64,2048]{1,0:T(8,128)(2,1)S(1)}, u32[]{:S(2)}, u32[]{:S(2)}) collective-permute-start(bf16[64,2048]{1,0:T(8,128)(2,1)S(1)} %get-tuple-element.19), channel_id=1, source_target_pairs={{3,2},{7,6},{11,10},{15,14},{19,18},{23,22},{27,26},{31,30}} | collective-permute-start | bytes 786440 | tf_op jit(solution)/shard_map/ppermute | solution.py:57
  27.8 11.5 %collective-permute-start.3 = (bf16[64,2048]{1,0:T(8,128)(2,1)S(1)}, bf16[64,2048]{1,0:T(8,128)(2,1)S(1)}, u32[]{:S(2)}, u32[]{:S(2)}) collective-permute-start(bf16[64,2048]{1,0:T(8,128)(2,1)S(1)} %add_convert_fusion.7), channel_id=1, source_target_pairs={{0,1},{1,2},{4,5},{5,6},{8,9},{9,10},{12,13},{13,14},{16,17},{17,1... | collective-permute-start | bytes 786440 | tf_op jit(solution)/shard_map/ppermute | solution.py:56
  33.8 11.4 %collective-permute-start.9 = (bf16[64,2048]{1,0:T(8,128)(2,1)S(1)}, bf16[64,2048]{1,0:T(8,128)(2,1)S(1)}, u32[]{:S(2)}, u32[]{:S(2)}) collective-permute-start(bf16[64,2048]{1,0:T(8,128)(2,1)S(1)} %add_convert_fusion.3), channel_id=1, source_target_pairs={{0,1},{1,2},{4,5},{5,6},{8,9},{9,10},{12,13},{13,14},{16,17},{17,1... | collective-permute-start | bytes 786440 | tf_op jit(solution)/shard_map/ppermute | solution.py:56
  39.5 11.9 %collective-permute-start.6 = (bf16[64,2048]{1,0:T(8,128)(2,1)S(1)}, bf16[64,2048]{1,0:T(8,128)(2,1)S(1)}, u32[]{:S(2)}, u32[]{:S(2)}) collective-permute-start(bf16[64,2048]{1,0:T(8,128)(2,1)S(1)} %get-tuple-element.13), channel_id=1, source_target_pairs={{3,2},{2,1},{7,6},{6,5},{11,10},{10,9},{15,14},{14,13},{19,18},{18... | collective-permute-start | bytes 786440 | tf_op jit(solution)/shard_map/ppermute | solution.py:57
  40.1 14.0 %collective-permute-start.4 = (bf16[64,2048]{1,0:T(8,128)(2,1)S(1)}, bf16[64,2048]{1,0:T(8,128)(2,1)S(1)}, u32[]{:S(2)}, u32[]{:S(2)}) collective-permute-start(bf16[64,2048]{1,0:T(8,128)(2,1)S(1)} %get-tuple-element.12), channel_id=1, source_target_pairs={{0,1},{1,2},{2,3},{4,5},{5,6},{6,7},{8,9},{9,10},{10,11},{12,13},{... | collective-permute-start | bytes 786440 | tf_op jit(solution)/shard_map/ppermute | solution.py:56
  45.3 7.4 %collective-permute-start.12 = (bf16[64,2048]{1,0:T(8,128)(2,1)S(1)}, bf16[64,2048]{1,0:T(8,128)(2,1)S(1)}, u32[]{:S(2)}, u32[]{:S(2)}) collective-permute-start(bf16[64,2048]{1,0:T(8,128)(2,1)S(1)} %get-tuple-element.17), channel_id=1, source_target_pairs={{3,2},{2,1},{7,6},{6,5},{11,10},{10,9},{15,14},{14,13},{19,18},{18... | collective-permute-start | bytes 786440 | tf_op jit(solution)/shard_map/ppermute | solution.py:57
  46.0 19.6 %copy-start = (bf16[64,4096]{1,0:T(8,128)(2,1)S(1)}, bf16[64,4096]{1,0:T(8,128)(2,1)}, u32[]{:S(2)}) copy-start(bf16[64,4096]{1,0:T(8,128)(2,1)} %param.7) | copy-start | bytes 1572868
  46.0 19.6 %copy-start.2 = (f32[4096]{0:T(1024)S(1)}, f32[4096]{0:T(1024)}, u32[]{:S(2)}) copy-start(f32[4096]{0:T(1024)} %param.8) | copy-start | bytes 49156
  46.0 16.7 %collective-permute-start.10 = (bf16[64,2048]{1,0:T(8,128)(2,1)S(1)}, bf16[64,2048]{1,0:T(8,128)(2,1)S(1)}, u32[]{:S(2)}, u32[]{:S(2)}) collective-permute-start(bf16[64,2048]{1,0:T(8,128)(2,1)S(1)} %get-tuple-element.16), channel_id=1, source_target_pairs={{0,1},{1,2},{2,3},{4,5},{5,6},{6,7},{8,9},{9,10},{10,11},{12,13},{... | collective-permute-start | bytes 786440 | tf_op jit(solution)/shard_map/ppermute | solution.py:56
  51.4 11.2 %collective-permute-start.7 = (bf16[64,2048]{1,0:T(8,128)(2,1)S(1)}, bf16[64,2048]{1,0:T(8,128)(2,1)S(1)}, u32[]{:S(2)}, u32[]{:S(2)}) collective-permute-start(bf16[64,2048]{1,0:T(8,128)(2,1)S(1)} %add_convert_fusion.4), channel_id=1, source_target_pairs={{3,2},{2,1},{1,0},{7,6},{6,5},{5,4},{11,10},{10,9},{9,8},{15,14},{... | collective-permute-start | bytes 786440 | tf_op jit(solution)/shard_map/ppermute | solution.py:57
  52.8 12.7 %collective-permute-start.13 = (bf16[64,2048]{1,0:T(8,128)(2,1)S(1)}, bf16[64,2048]{1,0:T(8,128)(2,1)S(1)}, u32[]{:S(2)}, u32[]{:S(2)}) collective-permute-start(bf16[64,2048]{1,0:T(8,128)(2,1)S(1)} %add_convert_fusion), channel_id=1, source_target_pairs={{3,2},{2,1},{1,0},{7,6},{6,5},{5,4},{11,10},{10,9},{9,8},{15,14},{... | collective-permute-start | bytes 786440 | tf_op jit(solution)/shard_map/ppermute | solution.py:57
  66.0 2.7 %collective-permute-start.14 = (f32[4096]{0:T(1024)S(1)}, f32[4096]{0:T(1024)S(1)}, u32[]{:S(2)}, u32[]{:S(2)}) collective-permute-start(f32[4096]{0:T(1024)S(1)} %get-tuple-element.8), channel_id=1, source_target_pairs={{0,4},{4,0},{8,12},{12,8},{16,20},{20,16},{24,28},{28,24},{1,5},{5... | collective-permute-start | bytes 49160 | tf_op jit(solution)/shard_map/ppermute | solution.py:34
  66.1 4.7 %collective-permute-start.20 = (f32[5,1024]{1,0:T(8,128)S(1)}, f32[5,1024]{1,0:T(8,128)S(1)}, u32[]{:S(2)}, u32[]{:S(2)}) collective-permute-start(f32[5,1024]{1,0:T(8,128)S(1)} %add.227), channel_id=1, source_target_pairs={{0,8},{4,12},{8,0},{12,4},{16,24},{20,28},{24,16},{28,20},{1,9},{5... | collective-permute-start | bytes 61448 | tf_op jit(solution)/shard_map/ppermute | solution.py:34
  68.8 4.9 %collective-permute-start.15 = (f32[4096]{0:T(1024)S(1)}, f32[4096]{0:T(1024)S(1)}, u32[]{:S(2)}, u32[]{:S(2)}) collective-permute-start(f32[4096]{0:T(1024)S(1)} %add.222), channel_id=1, source_target_pairs={{0,8},{4,12},{8,0},{12,4},{16,24},{20,28},{24,16},{28,20},{1,9},{5... | collective-permute-start | bytes 49160 | tf_op jit(solution)/shard_map/ppermute | solution.py:34
  70.8 4.9 %collective-permute-start.21 = (f32[5,1024]{1,0:T(8,128)S(1)}, f32[5,1024]{1,0:T(8,128)S(1)}, u32[]{:S(2)}, u32[]{:S(2)}) collective-permute-start(f32[5,1024]{1,0:T(8,128)S(1)} %add.228), channel_id=1, source_target_pairs={{0,16},{4,20},{8,24},{12,28},{16,0},{20,4},{24,8},{28,12},{1,17},{... | collective-permute-start | bytes 61448 | tf_op jit(solution)/shard_map/ppermute | solution.py:34
  73.7 3.8 %collective-permute-start.16 = (f32[4096]{0:T(1024)S(1)}, f32[4096]{0:T(1024)S(1)}, u32[]{:S(2)}, u32[]{:S(2)}) collective-permute-start(f32[4096]{0:T(1024)S(1)} %add.223), channel_id=1, source_target_pairs={{0,16},{4,20},{8,24},{12,28},{16,0},{20,4},{24,8},{28,12},{1,17},{... | collective-permute-start | bytes 49160 | tf_op jit(solution)/shard_map/ppermute | solution.py:34
  77.5 3.7 %collective-permute-start.17 = (f32[4096]{0:T(1024)S(1)}, f32[4096]{0:T(1024)S(1)}, u32[]{:S(2)}, u32[]{:S(2)}) collective-permute-start(f32[4096]{0:T(1024)S(1)} %add.224), channel_id=1, source_target_pairs={{0,1},{1,0},{2,3},{3,2},{4,5},{5,4},{6,7},{7,6},{8,9},{9,8},{10,11... | collective-permute-start | bytes 49160 | tf_op jit(solution)/shard_map/ppermute | solution.py:34
  81.2 4.6 %collective-permute-start.18 = (f32[4096]{0:T(1024)S(1)}, f32[4096]{0:T(1024)S(1)}, u32[]{:S(2)}, u32[]{:S(2)}) collective-permute-start(f32[4096]{0:T(1024)S(1)} %add.225), channel_id=1, source_target_pairs={{0,2},{1,3},{2,0},{3,1},{4,6},{5,7},{6,4},{7,5},{8,10},{9,11},{10,... | collective-permute-start | bytes 49160 | tf_op jit(solution)/shard_map/ppermute | solution.py:34
  (2 other events, 17.3 us)

commit v2 on v1

--- a/solution.py
+++ b/solution.py
@@ -31,36 +31,45 @@
         return lax.psum(value, axis)
     step = 1
     while step < size:
-        value = value + lax.ppermute(value, axis, [(i, i ^ step) for i in range(size)])
+        arrived = lax.ppermute(value, axis, [(i, i ^ step) for i in range(size)])
+        value = value + arrived
         step *= 2
     return value
 
 
-def line_scatter_parts(part, axis):
+def line_scatter(parts, axis):
     size = lax.axis_size(axis)
     place = lax.axis_index(axis)
-    rows = part.shape[0] // size
+    rows = parts[0].shape[0] // size
 
-    def block(index):
-        return lax.dynamic_slice_in_dim(part, jnp.clip(index, 0, size - 1) * rows, rows, 0)
+    def block(part, index):
+        return lax.dynamic_slice_in_dim(part, index * rows, rows, 0)
 
-    def joined(own, arrived):
-        if arrived is None:
-            return own
-        return (own.astype(jnp.float32) + arrived.astype(jnp.float32)).astype(part.dtype)
-
-    right = left = None
-    for hop in range(1, size):
-        send_right = joined(block(size - hop + place), right)
-        send_left = joined(block(hop - size + place), left)
-        right = lax.ppermute(send_right, axis, [(i, i + 1) for i in range(hop)])
-        left = lax.ppermute(send_left, axis, [(size - 1 - i, size - 2 - i) for i in range(hop)])
-        if hop < size - 1:
-            yield None
-    total = block(place).astype(jnp.float32)
-    if right is not None:
-        total = total + right.astype(jnp.float32) + left.astype(jnp.float32)
-    yield total
+    sums = [block(part, place).astype(jnp.float32) for part in parts]
+    last = [jnp.zeros(total.shape, part.dtype) for total, part in zip(sums, parts)]
+    sent = list(last)
+    first = None
+    for target in range(size - 1, 0, -1):
+        for index, part in enumerate(parts):
+            moving = None
+            for hop in range(target):
+                own = block(part, jnp.where(place == hop, target, size - 1 - target))
+                if moving is None:
+                    moving = lax.optimization_barrier(own)
+                else:
+                    moving = (own.astype(jnp.float32) + moving.astype(jnp.float32)).astype(part.dtype)
+                if target == 1:
+                    sent[index] = moving
+                moving = lax.ppermute(
+                    moving, axis, [(hop, hop + 1), (size - 1 - hop, size - 2 - hop)]
+                )
+                if first is None:
+                    first = moving
+            if target > 1:
+                sums[index] = sums[index] + moving.astype(jnp.float32)
+            else:
+                last[index] = moving
+    return sums, last, sent, first
 
 
 CHUNKS = 2
@@ -70,6 +79,7 @@
     count_tok = conv_in.shape[0]
     tap_count = conv_weight.shape[0]
     edge_rows = tap_count - 1
+    size = lax.axis_size("tp")
     earlier = from_behind(conv_in[count_tok - edge_rows :], "ctx", 1)
     later = from_behind(jnp.concatenate([conv_in[:edge_rows], act_grad[:edge_rows]], 0), "ctx", -1)
     later_in, later_grad = later[:edge_rows], later[edge_rows:]
@@ -86,10 +96,10 @@
             for index in range(tap_count)
         )
     ).astype(jnp.bfloat16)
-    in_grad = lax.optimization_barrier(in_grad)
+    in_grad, pre_grad, padded = lax.optimization_barrier((in_grad, pre_grad, padded))
     width = proj_weight.shape[0]
     chunk = width // CHUNKS
-    streams = []
+    parts = []
     for index in range(CHUNKS):
         part = lax.dot_general(
             in_grad,
@@ -97,11 +107,10 @@
             (((1,), (1,)), ((), ())),
             preferred_element_type=jnp.float32,
         ).astype(jnp.bfloat16)
-        streams.append(line_scatter_parts(lax.optimization_barrier(part), "tp"))
-    sums = [None] * CHUNKS
-    for _ in range(max(lax.axis_size("tp") - 1, 1)):
-        for index in range(CHUNKS):
-            sums[index] = next(streams[index])
+        parts.append(lax.optimization_barrier(part))
+    sums, last, sent, first = line_scatter(parts, "tp")
+    beside = lax.ppermute(hidden_in, "tp", [(1, 0), (size - 2, size - 1)])
+    pre_grad, padded, hidden_in, _ = lax.optimization_barrier((pre_grad, padded, hidden_in, first))
     taps_part = jnp.stack(
         [
             jnp.sum(pre_grad * padded[edge_rows - index : edge_rows - index + count_tok], 0)
@@ -112,12 +121,29 @@
     )
     taps_all = xor_sum(taps_part, "ctx")
     taps_grad, bias_grad = taps_all[:tap_count], taps_all[tap_count]
-    normalized_gradient = jnp.concatenate(sums, 1)
+
+    def rms_of(hidden):
+        return jnp.sqrt(jnp.mean(hidden * hidden, -1, keepdims=True) + 1e-05)
+
     hidden_state = hidden_in.astype(jnp.float32)
-    root_mean_square = jnp.sqrt(jnp.mean(hidden_state * hidden_state, -1, keepdims=True) + 1e-05)
+    root_mean_square = rms_of(hidden_state)
     normalized_input = hidden_state / root_mean_square
-    norm_gain_gradient = xor_sum(
-        xor_sum(jnp.sum(normalized_gradient * normalized_input, 0), "ctx"), "tp"
+    beside = beside.astype(jnp.float32)
+    normalized_beside = beside / rms_of(beside)
+    gain_part = jnp.concatenate(
+        [
+            jnp.sum(
+                sums[index] * normalized_input[:, index * chunk : (index + 1) * chunk]
+                + sent[index].astype(jnp.float32)
+                * normalized_beside[:, index * chunk : (index + 1) * chunk],
+                0,
+            )
+            for index in range(CHUNKS)
+        ]
+    )
+    norm_gain_gradient = xor_sum(xor_sum(gain_part, "ctx"), "tp")
+    normalized_gradient = jnp.concatenate(
+        [total + arrived.astype(jnp.float32) for total, arrived in zip(sums, last)], 1
     )
     scaled_gradient = norm_gain[None, :] * normalized_gradient
     mean_correction = jnp.mean(scaled_gradient * normalized_input, -1, keepdims=True)

time: 87.2 us -> 91.4 us (1.048)
  other arithmetic: 7.13 us -> 14.6 us
  matrix products: 6.95 us -> 4.9 us
  local copies, waits for them, and re-layouts: 3.79 us -> 5.11 us
  waiting for transfers between devices: 21.1 us -> 19.8 us
  starting transfers between devices: 46.5 us -> 45.2 us
    convert_element_type x6 -> x4, other arithmetic: 0.54 us -> 5.22 us  [line_scatter(): (own.astype(jnp.float32) + moving.astype(jnp.float32)).astype(part.dtype)]
    dot_general x2, matrix products: 6.95 us -> 4.9 us  [on_device(): lax.dot_general(in_grad, proj_weight[index * chunk:(index + 1) * chunk],...]
    ppermute x20 -> x21, starting transfers between devices: 42.8 us -> 40.8 us  [the longest x12 23.6 us: line_scatter(): lax.ppermute(moving, axis, [(hop, hop + 1), (size - 1 - hop, size - 2 - h...]
    mul x1 -> x2, other arithmetic: 0.05 us -> 1.71 us  [grad_of(): cotangent.astype(jnp.float32) * sigmoid_v]
    div x0 -> x2, other arithmetic: none -> 1.27 us  [the longest x1 1.12 us: on_device(): normalized_input = hidden_state / root_mean_square]
    ppermute x20 -> x21, waiting for transfers between devices: 21 us -> 19.8 us  [the longest x12 13 us: line_scatter(): lax.ppermute(moving, axis, [(hop, hop + 1), (size - 1 - hop, size - 2 - h...]
    dynamic_slice x2 -> x1, local copies, waits for them, and re-layouts: 0.1 us -> 1.09 us  [block(): return lax.dynamic_slice_in_dim(part, index * rows, rows, 0)]
    reduce_sum x2 -> x4, other arithmetic: 1.68 us -> 2.41 us  [the longest x1 1.62 us: on_device(): jnp.sum(sums[index] * normalized_input[:, index * chunk:(index + 1) * chu...]
  transfers between devices with their start and end apart: 22 -> 23, of which waited for: 9 -> 9; matrix products, arithmetic and copies ran while one was open for 19% -> 17% of each run, Pallas kernels for 0% -> 0%
where the time goes in v2:
time: 91.4 us; the launch traced here: 90.7 us
  starting transfers between devices  45.2 us (49%)
  waiting for transfers between devices  19.8 us (22%)
  other arithmetic  14.6 us (16%)
  local copies, waits for them, and re-layouts  5.11 us (6%)
  matrix products  4.9 us (5%)
  between operations  1.1 us (1%)
    ppermute x12, starting transfers between devices, line_scatter(): lax.ppermute(moving, axis, [(hop, hop + 1), (size - 1 - hop, size - 2 - h...  23.6 us
    ppermute x8, starting transfers between devices, xor_sum(): arrived = lax.ppermute(value, axis, [(i, i ^ step) for i in range(size)])  15.9 us
    ppermute x12, waiting for transfers between devices, line_scatter(): lax.ppermute(moving, axis, [(hop, hop + 1), (size - 1 - hop, size - 2 - h...  13 us
    ppermute x8, waiting for transfers between devices, xor_sum(): arrived = lax.ppermute(value, axis, [(i, i ^ step) for i in range(size)])  6.81 us
    convert_element_type x4, other arithmetic, line_scatter(): (own.astype(jnp.float32) + moving.astype(jnp.float32)).astype(part.dtype)  5.22 us
    dot_general x2, matrix products, on_device(): lax.dot_general(in_grad, proj_weight[index * chunk:(index + 1) * chunk],...  4.9 us
    ppermute x2, starting transfers between devices, from_behind(): return lax.ppermute(block, axis, route)  4.32 us
  transfers between devices with their start and end apart: 23, of which 9 were waited for; matrix products, arithmetic and copies ran while one was open for 17% of the time, Pallas kernels for 0%

profile of v2, /device:TPU:0, one launch (start us, length us, event | category | flops | bytes accessed | tf_op | source)
XLA Modules:
  0.0 90.7 jit_solution(8209664619779089292)
XLA Ops:
  2.2 1.3 %collective-permute-start.1 = (bf16[6,1024]{1,0:T(8,128)(2,1)S(1)}, bf16[6,1024]{1,0:T(8,128)(2,1)S(1)}, u32[]{:S(2)}, u32[]{:S(2)}) collective-permute-start(bf16[6,1024]{1,0:T(8,128)(2,1)S(1)} %pad_maximum_fusion.1), channel_id=1, source_target_pairs={{4,0},{8,4},{12,8},{16,12},{20,16},{24,20},{28,24},{5,1},{9,5},{13... | collective-permute-start | bytes 36872 | tf_op jit(solution)/shard_map/ppermute | solution.py:10
  3.5 3.0 %collective-permute-start = (bf16[3,1024]{1,0:T(4,128)(2,1)S(1)}, bf16[3,1024]{1,0:T(4,128)(2,1)S(1)}, u32[]{:S(2)}, u32[]{:S(2)}) collective-permute-start(bf16[3,1024]{1,0:T(4,128)(2,1)S(1)} %get-tuple-element.35), channel_id=1, source_target_pairs={{0,4},{4,8},{8,12},{12,16},{16,20},{20,24},{24,28},{1,5},{5,9},{9,... | collective-permute-start | bytes 18440 | tf_op jit(solution)/shard_map/ppermute | solution.py:10
  8.7 1.7 %add_multiply_fusion = f32[256,1024]{1,0:T(8,128)S(1)} fusion(f32[259,1024]{1,0:T(8,128)S(1)} %maximum_convert_fusion, bf16[256,1024]{1,0:T(8,128)(2,1)S(1)} %copy-done.6, f32[1024]{0:T(1024)S(1)} %bitcast.18, f32[1024]{0:T(1024)S(1)} %bitcast.21, f32[1024]{0:T(1024)S(1)} %bitcast.15, f32[1024]{0:T(1024)} %param.12, f32[1024]{0:T(1024)S(1)} %bitcast.12), kind=kLoop, calls=%fused_computation.39 | loop fusion | flops 4456448 | bytes 5787648 | tf_op jit(solution)/shard_map/mul | solution.py:25
  10.9 3.6 %fusion.4 = bf16[256,2048]{1,0:T(8,128)(2,1)S(1)} fusion(bf16[256,1024]{1,0:T(8,128)(2,1)S(1)} %fusion.16, bf16[4096,1024]{1,0:T(8,128)(2,1)} %param.9), kind=kOutput, calls=%fused_computation.4 | convolution fusion | flops 1074266112 | bytes 5767168 | tf_op jit(solution)/shard_map/dot_general | solution.py:104
  17.3 5.7 %collective-permute-start.2 = (bf16[64,2048]{1,0:T(8,128)(2,1)}, bf16[64,2048]{1,0:T(8,128)(2,1)}, u32[]{:S(2)}, u32[]{:S(2)}) collective-permute-start(bf16[64,2048]{1,0:T(8,128)(2,1)} %get-tuple-element.43), channel_id=1, source_target_pairs={{0,1},{3,2},{4,5},{7,6},{8,9},{11,10},{12,13},{15,14},{16,17},{19,... | collective-permute-start | bytes 786440 | tf_op jit(solution)/shard_map/ppermute | solution.py:63
  24.3 5.3 %collective-permute-start.8 = (bf16[64,2048]{1,0:T(8,128)(2,1)}, bf16[64,2048]{1,0:T(8,128)(2,1)}, u32[]{:S(2)}, u32[]{:S(2)}) collective-permute-start(bf16[64,2048]{1,0:T(8,128)(2,1)} %get-tuple-element.32), channel_id=1, source_target_pairs={{0,1},{3,2},{4,5},{7,6},{8,9},{11,10},{12,13},{15,14},{16,17},{19,... | collective-permute-start | bytes 786440 | tf_op jit(solution)/shard_map/ppermute | solution.py:63
  29.6 2.0 %collective-permute-start.11 = (bf16[64,2048]{1,0:T(8,128)(2,1)}, bf16[64,2048]{1,0:T(8,128)(2,1)}, u32[]{:S(2)}, u32[]{:S(2)}) collective-permute-start(bf16[64,2048]{1,0:T(8,128)(2,1)} %get-tuple-element.34), channel_id=1, source_target_pairs={{0,1},{3,2},{4,5},{7,6},{8,9},{11,10},{12,13},{15,14},{16,17},{19,... | collective-permute-start | bytes 786440 | tf_op jit(solution)/shard_map/ppermute | solution.py:63
  31.6 2.0 %collective-permute-start.5 = (bf16[64,2048]{1,0:T(8,128)(2,1)}, bf16[64,2048]{1,0:T(8,128)(2,1)}, u32[]{:S(2)}, u32[]{:S(2)}) collective-permute-start(bf16[64,2048]{1,0:T(8,128)(2,1)} %get-tuple-element.41), channel_id=1, source_target_pairs={{0,1},{3,2},{4,5},{7,6},{8,9},{11,10},{12,13},{15,14},{16,17},{19,... | collective-permute-start | bytes 786440 | tf_op jit(solution)/shard_map/ppermute | solution.py:63
  33.6 2.0 %collective-permute-start.13 = (bf16[64,2048]{1,0:T(8,128)(2,1)S(1)}, bf16[64,2048]{1,0:T(8,128)(2,1)}, u32[]{:S(2)}, u32[]{:S(2)}) collective-permute-start(bf16[64,2048]{1,0:T(8,128)(2,1)S(1)} %get-tuple-element.33), channel_id=1, source_target_pairs={{0,1},{3,2},{4,5},{7,6},{8,9},{11,10},{12,13},{15,14},{16,17},{19,... | collective-permute-start | bytes 786440 | tf_op jit(solution)/shard_map/ppermute | solution.py:63
  36.9 1.8 %add_convert_fusion.5 = bf16[64,2048]{1,0:T(8,128)(2,1)} fusion(bf16[64,2048]{1,0:T(8,128)(2,1)} %collective-permute-done.2, bf16[256,2048]{1,0:T(8,128)(2,1)} %copy-done.2, s32[]{:T(128)S(6)} %select_n.57), kind=kLoop, calls=%fused_computation.58 | loop fusion | flops 524288 | bytes 786436 | tf_op jit(solution)/shard_map/convert_element_type | solution.py:60
  40.8 1.3 %collective-permute-start.7 = (bf16[64,2048]{1,0:T(8,128)(2,1)}, bf16[64,2048]{1,0:T(8,128)(2,1)S(1)}, u32[]{:S(2)}, u32[]{:S(2)}) collective-permute-start(bf16[64,2048]{1,0:T(8,128)(2,1)} %get-tuple-element.42), channel_id=1, source_target_pairs={{0,1},{3,2},{4,5},{7,6},{8,9},{11,10},{12,13},{15,14},{16,17},{19,... | collective-permute-start | bytes 786440 | tf_op jit(solution)/shard_map/ppermute | solution.py:63
  45.1 1.3 %collective-permute-start.10 = (bf16[64,2048]{1,0:T(8,128)(2,1)S(1)}, bf16[64,2048]{1,0:T(8,128)(2,1)S(1)}, u32[]{:S(2)}, u32[]{:S(2)}) collective-permute-start(bf16[64,2048]{1,0:T(8,128)(2,1)S(1)} %get-tuple-element.30), channel_id=1, source_target_pairs={{2,3},{1,0},{6,7},{5,4},{10,11},{9,8},{14,15},{13,12},{18,19},{17,... | collective-permute-start | bytes 786440 | tf_op jit(solution)/shard_map/ppermute | solution.py:63
  50.2 2.4 %collective-permute-done.13 = bf16[64,2048]{1,0:T(8,128)(2,1)} collective-permute-done((bf16[64,2048]{1,0:T(8,128)(2,1)S(1)}, bf16[64,2048]{1,0:T(8,128)(2,1)}, u32[]{:S(2)}, u32[]{:S(2)}) %collective-permute-start.13) | collective-permute-done | bytes 262176 | tf_op jit(solution)/shard_map/ppermute | solution.py:63
  53.4 4.5 %collective-permute-done.7 = bf16[64,2048]{1,0:T(8,128)(2,1)S(1)} collective-permute-done((bf16[64,2048]{1,0:T(8,128)(2,1)}, bf16[64,2048]{1,0:T(8,128)(2,1)S(1)}, u32[]{:S(2)}, u32[]{:S(2)}) %collective-permute-start.7) | collective-permute-done | bytes 262176 | tf_op jit(solution)/shard_map/ppermute | solution.py:63
  57.9 2.4 %collective-permute-start.21 = (f32[5,1024]{1,0:T(8,128)S(1)}, f32[5,1024]{1,0:T(8,128)S(1)}, u32[]{:S(2)}, u32[]{:S(2)}) collective-permute-start(f32[5,1024]{1,0:T(8,128)S(1)} %add.210), channel_id=1, source_target_pairs={{0,8},{4,12},{8,0},{12,4},{16,24},{20,28},{24,16},{28,20},{1,9},{5... | collective-permute-start | bytes 61448 | tf_op jit(solution)/shard_map/ppermute | solution.py:34
  60.3 5.4 %collective-permute-done.4 = bf16[64,2048]{1,0:T(8,128)(2,1)S(1)} collective-permute-done((bf16[64,2048]{1,0:T(8,128)(2,1)S(1)}, bf16[64,2048]{1,0:T(8,128)(2,1)S(1)}, u32[]{:S(2)}, u32[]{:S(2)}) %collective-permute-start.4) | collective-permute-done | bytes 262176 | tf_op jit(solution)/shard_map/ppermute | solution.py:63
  65.7 1.6 %fusion.28 = (f32[2048]{0:T(1024)S(1)}, f32[2048]{0:T(1024)S(1)}, f32[64,2048]{1,0:T(8,128)S(1)}, f32[64,2048]{1,0:T(8,128)S(1)}) fusion(f32[64,4096]{1,0:T(8,128)S(1)} %convert_divide_fusion, f32[64,4096]{1,0:T(8,128)S(1)} %copy-done.1, bf16[64,2048]{1,0:T(8,128)(2,1)S(1)} %copy-done.5, bf16[64,2048]{1,0:T(8,128)(2,1)S(1)} %collective-permute-done.6, ...), kind=kLoop, calls=%fused_computation.47 | loop fusion | flops 3141632 | bytes 5783556 | tf_op jit(solution)/shard_map/reduce_sum | solution.py:135
  67.4 5.0 %collective-permute-start.22 = (f32[5,1024]{1,0:T(8,128)S(1)}, f32[5,1024]{1,0:T(8,128)S(1)}, u32[]{:S(2)}, u32[]{:S(2)}) collective-permute-start(f32[5,1024]{1,0:T(8,128)S(1)} %add.211), channel_id=1, source_target_pairs={{0,16},{4,20},{8,24},{12,28},{16,0},{20,4},{24,8},{28,12},{1,17},{... | collective-permute-start | bytes 61448 | tf_op jit(solution)/shard_map/ppermute | solution.py:34
  72.4 2.0 %collective-permute-done.22 = f32[5,1024]{1,0:T(8,128)S(1)} collective-permute-done((f32[5,1024]{1,0:T(8,128)S(1)}, f32[5,1024]{1,0:T(8,128)S(1)}, u32[]{:S(2)}, u32[]{:S(2)}) %collective-permute-start.22) | collective-permute-done | bytes 20512 | tf_op jit(solution)/shard_map/ppermute | solution.py:34
  76.2 1.4 %collective-permute-start.17 = (f32[4096]{0:T(1024)S(1)}, f32[4096]{0:T(1024)S(1)}, u32[]{:S(2)}, u32[]{:S(2)}) collective-permute-start(f32[4096]{0:T(1024)S(1)} %add.206), channel_id=1, source_target_pairs={{0,16},{4,20},{8,24},{12,28},{16,0},{20,4},{24,8},{28,12},{1,17},{... | collective-permute-start | bytes 49160 | tf_op jit(solution)/shard_map/ppermute | solution.py:34
  78.0 1.9 %collective-permute-done.17 = f32[4096]{0:T(1024)S(1)} collective-permute-done((f32[4096]{0:T(1024)S(1)}, f32[4096]{0:T(1024)S(1)}, u32[]{:S(2)}, u32[]{:S(2)}) %collective-permute-start.17) | collective-permute-done | bytes 16416 | tf_op jit(solution)/shard_map/ppermute | solution.py:34
  79.9 3.7 %collective-permute-start.18 = (f32[4096]{0:T(1024)S(1)}, f32[4096]{0:T(1024)S(1)}, u32[]{:S(2)}, u32[]{:S(2)}) collective-permute-start(f32[4096]{0:T(1024)S(1)} %add.207), channel_id=1, source_target_pairs={{0,1},{1,0},{2,3},{3,2},{4,5},{5,4},{6,7},{7,6},{8,9},{9,8},{10,11... | collective-permute-start | bytes 49160 | tf_op jit(solution)/shard_map/ppermute | solution.py:34
  83.6 1.7 %collective-permute-done.18 = f32[4096]{0:T(1024)S(1)} collective-permute-done((f32[4096]{0:T(1024)S(1)}, f32[4096]{0:T(1024)S(1)}, u32[]{:S(2)}, u32[]{:S(2)}) %collective-permute-start.18) | collective-permute-done | bytes 16416 | tf_op jit(solution)/shard_map/ppermute | solution.py:34
  85.3 3.0 %collective-permute-start.19 = (f32[4096]{0:T(1024)S(1)}, f32[4096]{0:T(1024)S(1)}, u32[]{:S(2)}, u32[]{:S(2)}) collective-permute-start(f32[4096]{0:T(1024)S(1)} %add.208), channel_id=1, source_target_pairs={{0,2},{1,3},{2,0},{3,1},{4,6},{5,7},{6,4},{7,5},{8,10},{9,11},{10,... | collective-permute-start | bytes 49160 | tf_op jit(solution)/shard_map/ppermute | solution.py:34
  (85 shorter events, 23.6 us)
Async XLA Ops:
  2.2 8.2 %collective-permute-start.1 = (bf16[6,1024]{1,0:T(8,128)(2,1)S(1)}, bf16[6,1024]{1,0:T(8,128)(2,1)S(1)}, u32[]{:S(2)}, u32[]{:S(2)}) collective-permute-start(bf16[6,1024]{1,0:T(8,128)(2,1)S(1)} %pad_maximum_fusion.1), channel_id=1, source_target_pairs={{4,0},{8,4},{12,8},{16,12},{20,16},{24,20},{28,24},{5,1},{9,5},{13... | collective-permute-start | bytes 36872 | tf_op jit(solution)/shard_map/ppermute | solution.py:10
  3.5 3.9 %collective-permute-start = (bf16[3,1024]{1,0:T(4,128)(2,1)S(1)}, bf16[3,1024]{1,0:T(4,128)(2,1)S(1)}, u32[]{:S(2)}, u32[]{:S(2)}) collective-permute-start(bf16[3,1024]{1,0:T(4,128)(2,1)S(1)} %get-tuple-element.35), channel_id=1, source_target_pairs={{0,4},{4,8},{8,12},{12,16},{16,20},{20,24},{24,28},{1,5},{5,9},{9,... | collective-permute-start | bytes 18440 | tf_op jit(solution)/shard_map/ppermute | solution.py:10
  17.3 16.2 %collective-permute-start.2 = (bf16[64,2048]{1,0:T(8,128)(2,1)}, bf16[64,2048]{1,0:T(8,128)(2,1)}, u32[]{:S(2)}, u32[]{:S(2)}) collective-permute-start(bf16[64,2048]{1,0:T(8,128)(2,1)} %get-tuple-element.43), channel_id=1, source_target_pairs={{0,1},{3,2},{4,5},{7,6},{8,9},{11,10},{12,13},{15,14},{16,17},{19,... | collective-permute-start | bytes 786440 | tf_op jit(solution)/shard_map/ppermute | solution.py:63
  23.0 19.1 %collective-permute-start.14 = (bf16[64,4096]{1,0:T(8,128)(2,1)S(1)}, bf16[64,4096]{1,0:T(8,128)(2,1)S(1)}, u32[]{:S(2)}, u32[]{:S(2)}) collective-permute-start(bf16[64,4096]{1,0:T(8,128)(2,1)S(1)} %copy-done), channel_id=1, source_target_pairs={{1,0},{2,3},{5,4},{6,7},{9,8},{10,11},{13,12},{14,15},{17,16},{18,... | collective-permute-start | bytes 1572872 | tf_op jit(solution)/shard_map/ppermute | solution.py:112
  24.3 15.0 %collective-permute-start.8 = (bf16[64,2048]{1,0:T(8,128)(2,1)}, bf16[64,2048]{1,0:T(8,128)(2,1)}, u32[]{:S(2)}, u32[]{:S(2)}) collective-permute-start(bf16[64,2048]{1,0:T(8,128)(2,1)} %get-tuple-element.32), channel_id=1, source_target_pairs={{0,1},{3,2},{4,5},{7,6},{8,9},{11,10},{12,13},{15,14},{16,17},{19,... | collective-permute-start | bytes 786440 | tf_op jit(solution)/shard_map/ppermute | solution.py:63
  29.6 13.4 %collective-permute-start.11 = (bf16[64,2048]{1,0:T(8,128)(2,1)}, bf16[64,2048]{1,0:T(8,128)(2,1)}, u32[]{:S(2)}, u32[]{:S(2)}) collective-permute-start(bf16[64,2048]{1,0:T(8,128)(2,1)} %get-tuple-element.34), channel_id=1, source_target_pairs={{0,1},{3,2},{4,5},{7,6},{8,9},{11,10},{12,13},{15,14},{16,17},{19,... | collective-permute-start | bytes 786440 | tf_op jit(solution)/shard_map/ppermute | solution.py:63
  31.6 15.5 %collective-permute-start.5 = (bf16[64,2048]{1,0:T(8,128)(2,1)}, bf16[64,2048]{1,0:T(8,128)(2,1)}, u32[]{:S(2)}, u32[]{:S(2)}) collective-permute-start(bf16[64,2048]{1,0:T(8,128)(2,1)} %get-tuple-element.41), channel_id=1, source_target_pairs={{0,1},{3,2},{4,5},{7,6},{8,9},{11,10},{12,13},{15,14},{16,17},{19,... | collective-permute-start | bytes 786440 | tf_op jit(solution)/shard_map/ppermute | solution.py:63
  33.6 19.1 %collective-permute-start.13 = (bf16[64,2048]{1,0:T(8,128)(2,1)S(1)}, bf16[64,2048]{1,0:T(8,128)(2,1)}, u32[]{:S(2)}, u32[]{:S(2)}) collective-permute-start(bf16[64,2048]{1,0:T(8,128)(2,1)S(1)} %get-tuple-element.33), channel_id=1, source_target_pairs={{0,1},{3,2},{4,5},{7,6},{8,9},{11,10},{12,13},{15,14},{16,17},{19,... | collective-permute-start | bytes 786440 | tf_op jit(solution)/shard_map/ppermute | solution.py:63
  39.3 1.4 %collective-permute-start.20 = (f32[5,1024]{1,0:T(8,128)S(1)}, f32[5,1024]{1,0:T(8,128)S(1)}, u32[]{:S(2)}, u32[]{:S(2)}) collective-permute-start(f32[5,1024]{1,0:T(8,128)S(1)} %stack.23), channel_id=1, source_target_pairs={{0,4},{4,0},{8,12},{12,8},{16,20},{20,16},{24,28},{28,24},{1,5},{5... | collective-permute-start | bytes 61448 | tf_op jit(solution)/shard_map/ppermute | solution.py:34
  40.8 17.2 %collective-permute-start.7 = (bf16[64,2048]{1,0:T(8,128)(2,1)}, bf16[64,2048]{1,0:T(8,128)(2,1)S(1)}, u32[]{:S(2)}, u32[]{:S(2)}) collective-permute-start(bf16[64,2048]{1,0:T(8,128)(2,1)} %get-tuple-element.42), channel_id=1, source_target_pairs={{0,1},{3,2},{4,5},{7,6},{8,9},{11,10},{12,13},{15,14},{16,17},{19,... | collective-permute-start | bytes 786440 | tf_op jit(solution)/shard_map/ppermute | solution.py:63
  42.1 1.8 %collective-permute-start.9 = (bf16[64,2048]{1,0:T(8,128)(2,1)S(1)}, bf16[64,2048]{1,0:T(8,128)(2,1)S(1)}, u32[]{:S(2)}, u32[]{:S(2)}) collective-permute-start(bf16[64,2048]{1,0:T(8,128)(2,1)S(1)} %add_convert_fusion.2), channel_id=1, source_target_pairs={{1,2},{2,1},{5,6},{6,5},{9,10},{10,9},{13,14},{14,13},{17,18},{18,... | collective-permute-start | bytes 786440 | tf_op jit(solution)/shard_map/ppermute | solution.py:63
  43.0 4.7 %collective-permute-start.3 = (bf16[64,2048]{1,0:T(8,128)(2,1)}, bf16[64,2048]{1,0:T(8,128)(2,1)S(1)}, u32[]{:S(2)}, u32[]{:S(2)}) collective-permute-start(bf16[64,2048]{1,0:T(8,128)(2,1)} %add_convert_fusion.5), channel_id=1, source_target_pairs={{1,2},{2,1},{5,6},{6,5},{9,10},{10,9},{13,14},{14,13},{17,18},{18,... | collective-permute-start | bytes 786440 | tf_op jit(solution)/shard_map/ppermute | solution.py:63
  45.1 15.2 %collective-permute-start.10 = (bf16[64,2048]{1,0:T(8,128)(2,1)S(1)}, bf16[64,2048]{1,0:T(8,128)(2,1)S(1)}, u32[]{:S(2)}, u32[]{:S(2)}) collective-permute-start(bf16[64,2048]{1,0:T(8,128)(2,1)S(1)} %get-tuple-element.30), channel_id=1, source_target_pairs={{2,3},{1,0},{6,7},{5,4},{10,11},{9,8},{14,15},{13,12},{18,19},{17,... | collective-permute-start | bytes 786440 | tf_op jit(solution)/shard_map/ppermute | solution.py:63
  47.1 13.2 %collective-permute-start.12 = (bf16[64,2048]{1,0:T(8,128)(2,1)S(1)}, bf16[64,2048]{1,0:T(8,128)(2,1)S(1)}, u32[]{:S(2)}, u32[]{:S(2)}) collective-permute-start(bf16[64,2048]{1,0:T(8,128)(2,1)S(1)} %get-tuple-element.31), channel_id=1, source_target_pairs={{1,2},{2,1},{5,6},{6,5},{9,10},{10,9},{13,14},{14,13},{17,18},{18,... | collective-permute-start | bytes 786440 | tf_op jit(solution)/shard_map/ppermute | solution.py:63
  48.9 16.8 %collective-permute-start.4 = (bf16[64,2048]{1,0:T(8,128)(2,1)S(1)}, bf16[64,2048]{1,0:T(8,128)(2,1)S(1)}, u32[]{:S(2)}, u32[]{:S(2)}) collective-permute-start(bf16[64,2048]{1,0:T(8,128)(2,1)S(1)} %get-tuple-element.25), channel_id=1, source_target_pairs={{2,3},{1,0},{6,7},{5,4},{10,11},{9,8},{14,15},{13,12},{18,19},{17,... | collective-permute-start | bytes 786440 | tf_op jit(solution)/shard_map/ppermute | solution.py:63
  52.6 13.1 %collective-permute-start.6 = (bf16[64,2048]{1,0:T(8,128)(2,1)S(1)}, bf16[64,2048]{1,0:T(8,128)(2,1)S(1)}, u32[]{:S(2)}, u32[]{:S(2)}) collective-permute-start(bf16[64,2048]{1,0:T(8,128)(2,1)S(1)} %get-tuple-element.26), channel_id=1, source_target_pairs={{1,2},{2,1},{5,6},{6,5},{9,10},{10,9},{13,14},{14,13},{17,18},{18,... | collective-permute-start | bytes 786440 | tf_op jit(solution)/shard_map/ppermute | solution.py:63
  53.4 24.2 %copy-start.7 = (f32[4096]{0:T(1024)S(1)}, f32[4096]{0:T(1024)}, u32[]{:S(2)}) copy-start(f32[4096]{0:T(1024)} %param.8) | copy-start | bytes 49156
  57.9 9.5 %collective-permute-start.21 = (f32[5,1024]{1,0:T(8,128)S(1)}, f32[5,1024]{1,0:T(8,128)S(1)}, u32[]{:S(2)}, u32[]{:S(2)}) collective-permute-start(f32[5,1024]{1,0:T(8,128)S(1)} %add.210), channel_id=1, source_target_pairs={{0,8},{4,12},{8,0},{12,4},{16,24},{20,28},{24,16},{28,20},{1,9},{5... | collective-permute-start | bytes 61448 | tf_op jit(solution)/shard_map/ppermute | solution.py:34
  67.3 5.1 %collective-permute-start.15 = (f32[4096]{0:T(1024)S(1)}, f32[4096]{0:T(1024)S(1)}, u32[]{:S(2)}, u32[]{:S(2)}) collective-permute-start(f32[4096]{0:T(1024)S(1)} %pad_maximum_fusion.2), channel_id=1, source_target_pairs={{0,4},{4,0},{8,12},{12,8},{16,20},{20,16},{24,28},{28,24},{1,5},{5... | collective-permute-start | bytes 49160 | tf_op jit(solution)/shard_map/ppermute | solution.py:34
  67.4 7.0 %collective-permute-start.22 = (f32[5,1024]{1,0:T(8,128)S(1)}, f32[5,1024]{1,0:T(8,128)S(1)}, u32[]{:S(2)}, u32[]{:S(2)}) collective-permute-start(f32[5,1024]{1,0:T(8,128)S(1)} %add.211), channel_id=1, source_target_pairs={{0,16},{4,20},{8,24},{12,28},{16,0},{20,4},{24,8},{28,12},{1,17},{... | collective-permute-start | bytes 61448 | tf_op jit(solution)/shard_map/ppermute | solution.py:34
  72.4 3.7 %collective-permute-start.16 = (f32[4096]{0:T(1024)S(1)}, f32[4096]{0:T(1024)S(1)}, u32[]{:S(2)}, u32[]{:S(2)}) collective-permute-start(f32[4096]{0:T(1024)S(1)} %fusion.33), channel_id=1, source_target_pairs={{0,8},{4,12},{8,0},{12,4},{16,24},{20,28},{24,16},{28,20},{1,9},{5... | collective-permute-start | bytes 49160 | tf_op jit(solution)/shard_map/ppermute | solution.py:34
  76.2 3.7 %collective-permute-start.17 = (f32[4096]{0:T(1024)S(1)}, f32[4096]{0:T(1024)S(1)}, u32[]{:S(2)}, u32[]{:S(2)}) collective-permute-start(f32[4096]{0:T(1024)S(1)} %add.206), channel_id=1, source_target_pairs={{0,16},{4,20},{8,24},{12,28},{16,0},{20,4},{24,8},{28,12},{1,17},{... | collective-permute-start | bytes 49160 | tf_op jit(solution)/shard_map/ppermute | solution.py:34
  79.9 5.4 %collective-permute-start.18 = (f32[4096]{0:T(1024)S(1)}, f32[4096]{0:T(1024)S(1)}, u32[]{:S(2)}, u32[]{:S(2)}) collective-permute-start(f32[4096]{0:T(1024)S(1)} %add.207), channel_id=1, source_target_pairs={{0,1},{1,0},{2,3},{3,2},{4,5},{5,4},{6,7},{7,6},{8,9},{9,8},{10,11... | collective-permute-start | bytes 49160 | tf_op jit(solution)/shard_map/ppermute | solution.py:34
  85.3 4.8 %collective-permute-start.19 = (f32[4096]{0:T(1024)S(1)}, f32[4096]{0:T(1024)S(1)}, u32[]{:S(2)}, u32[]{:S(2)}) collective-permute-start(f32[4096]{0:T(1024)S(1)} %add.208), channel_id=1, source_target_pairs={{0,2},{1,3},{2,0},{3,1},{4,6},{5,7},{6,4},{7,5},{8,10},{9,11},{10,... | collective-permute-start | bytes 49160 | tf_op jit(solution)/shard_map/ppermute | solution.py:34
  (10 other events, 83.0 us)

commit v3 on v2

--- a/solution.py
+++ b/solution.py
@@ -39,13 +39,13 @@
 
 def line_scatter(parts, axis):
     size = lax.axis_size(axis)
-    place = lax.axis_index(axis)
     rows = parts[0].shape[0] // size
+    places = [lax.optimization_barrier((lax.axis_index(axis), part))[0] for part in parts]
 
     def block(part, index):
         return lax.dynamic_slice_in_dim(part, index * rows, rows, 0)
 
-    sums = [block(part, place).astype(jnp.float32) for part in parts]
+    sums = [block(part, place).astype(jnp.float32) for part, place in zip(parts, places)]
     last = [jnp.zeros(total.shape, part.dtype) for total, part in zip(sums, parts)]
     sent = list(last)
     first = None
@@ -53,7 +53,7 @@
         for index, part in enumerate(parts):
             moving = None
             for hop in range(target):
-                own = block(part, jnp.where(place == hop, target, size - 1 - target))
+                own = block(part, jnp.where(places[index] == hop, target, size - 1 - target))
                 if moving is None:
                     moving = lax.optimization_barrier(own)
                 else:
@@ -82,6 +82,7 @@
     size = lax.axis_size("tp")
     earlier = from_behind(conv_in[count_tok - edge_rows :], "ctx", 1)
     later = from_behind(jnp.concatenate([conv_in[:edge_rows], act_grad[:edge_rows]], 0), "ctx", -1)
+    beside = lax.ppermute(hidden_in, "tp", [(1, 0), (size - 2, size - 1)])
     later_in, later_grad = later[:edge_rows], later[edge_rows:]
     padded = jnp.concatenate([earlier, conv_in], 0).astype(jnp.float32)
     preact = preact_of(padded, conv_weight, conv_bias, count_tok)
@@ -109,8 +110,9 @@
         ).astype(jnp.bfloat16)
         parts.append(lax.optimization_barrier(part))
     sums, last, sent, first = line_scatter(parts, "tp")
-    beside = lax.ppermute(hidden_in, "tp", [(1, 0), (size - 2, size - 1)])
-    pre_grad, padded, hidden_in, _ = lax.optimization_barrier((pre_grad, padded, hidden_in, first))
+    pre_grad, padded, hidden_in, beside, _ = lax.optimization_barrier(
+        (pre_grad, padded, hidden_in, beside, first)
+    )
     taps_part = jnp.stack(
         [
             jnp.sum(pre_grad * padded[edge_rows - index : edge_rows - index + count_tok], 0)
@@ -130,18 +132,19 @@
     normalized_input = hidden_state / root_mean_square
     beside = beside.astype(jnp.float32)
     normalized_beside = beside / rms_of(beside)
-    gain_part = jnp.concatenate(
-        [
-            jnp.sum(
-                sums[index] * normalized_input[:, index * chunk : (index + 1) * chunk]
-                + sent[index].astype(jnp.float32)
-                * normalized_beside[:, index * chunk : (index + 1) * chunk],
-                0,
-            )
-            for index in range(CHUNKS)
-        ]
-    )
-    norm_gain_gradient = xor_sum(xor_sum(gain_part, "ctx"), "tp")
+    sums = lax.optimization_barrier(sums)
+    gain_part = [
+        jnp.sum(
+            sums[index] * normalized_input[:, index * chunk : (index + 1) * chunk]
+            + sent[index].astype(jnp.float32)
+            * normalized_beside[:, index * chunk : (index + 1) * chunk],
+            0,
+        )
+        for index in range(CHUNKS)
+    ]
+    gain_part = lax.optimization_barrier(jnp.concatenate(gain_part))
+    gain_part, last = lax.optimization_barrier((xor_sum(gain_part, "ctx"), last))
+    norm_gain_gradient = xor_sum(gain_part, "tp")
     normalized_gradient = jnp.concatenate(
         [total + arrived.astype(jnp.float32) for total, arrived in zip(sums, last)], 1
     )

time: 91.4 us -> 109 us (1.19)
  waiting for transfers between devices: 19.8 us -> 31.4 us
  other arithmetic: 14.6 us -> 20.5 us
  starting transfers between devices: 45.2 us -> 39.4 us
  matrix products: 4.9 us -> 8.13 us
  local copies, waits for them, and re-layouts: 5.11 us -> 7.37 us
    ppermute x12, waiting for transfers between devices: 13 us -> 20.6 us  [line_scatter(): lax.ppermute(moving, axis, [(hop, hop + 1), (size - 1 - hop, size - 2 - h...]
    ppermute x8, starting transfers between devices: 15.9 us -> 8.69 us  [xor_sum(): arrived = lax.ppermute(value, axis, [(i, i ^ step) for i in range(size)])]
    ppermute x8, waiting for transfers between devices: 6.81 us -> 10.7 us  [xor_sum(): arrived = lax.ppermute(value, axis, [(i, i ^ step) for i in range(size)])]
    dot_general x2, matrix products: 4.9 us -> 8.13 us  [on_device(): lax.dot_general(in_grad, proj_weight[index * chunk:(index + 1) * chunk],...]
    add x0 -> x3, other arithmetic: none -> 3.15 us  [the longest x2 2.09 us: line_scatter(): sums[index] = sums[index] + moving.astype(jnp.float32)]
    div x1, other arithmetic: 0.15 us -> 2.18 us  [on_device(): normalized_beside = beside / rms_of(beside)]
    dynamic_slice x1 -> x2, local copies, waits for them, and re-layouts: 1.09 us -> 2.88 us  [block(): return lax.dynamic_slice_in_dim(part, index * rows, rows, 0)]
    ppermute x12, starting transfers between devices: 23.6 us -> 25.1 us  [line_scatter(): lax.ppermute(moving, axis, [(hop, hop + 1), (size - 1 - hop, size - 2 - h...]
  transfers between devices with their start and end apart: 23 -> 23, of which waited for: 9 -> 9; matrix products, arithmetic and copies ran while one was open for 17% -> 31% of each run, Pallas kernels for 0% -> 0%
where the time goes in v3:
time: 109 us; the launch traced here: 108 us
  starting transfers between devices  39.4 us (36%)
  waiting for transfers between devices  31.4 us (29%)
  other arithmetic  20.5 us (19%)
  matrix products  8.13 us (7%)
  local copies, waits for them, and re-layouts  7.37 us (7%)
    ppermute x12, starting transfers between devices, line_scatter(): lax.ppermute(moving, axis, [(hop, hop + 1), (size - 1 - hop, size - 2 - h...  25.1 us
    ppermute x12, waiting for transfers between devices, line_scatter(): lax.ppermute(moving, axis, [(hop, hop + 1), (size - 1 - hop, size - 2 - h...  20.6 us
    ppermute x8, waiting for transfers between devices, xor_sum(): arrived = lax.ppermute(value, axis, [(i, i ^ step) for i in range(size)])  10.7 us
    ppermute x8, starting transfers between devices, xor_sum(): arrived = lax.ppermute(value, axis, [(i, i ^ step) for i in range(size)])  8.69 us
    dot_general x2, matrix products, on_device(): lax.dot_general(in_grad, proj_weight[index * chunk:(index + 1) * chunk],...  8.13 us
    convert_element_type x4, other arithmetic, line_scatter(): (own.astype(jnp.float32) + moving.astype(jnp.float32)).astype(part.dtype)  6.18 us
    ppermute x2, starting transfers between devices, from_behind(): return lax.ppermute(block, axis, route)  4.32 us
    dynamic_slice x2, local copies, waits for them, and re-layouts, block(): return lax.dynamic_slice_in_dim(part, index * rows, rows, 0)  2.88 us
  transfers between devices with their start and end apart: 23, of which 9 were waited for; matrix products, arithmetic and copies ran while one was open for 31% of the time, Pallas kernels for 0%

profile of v3, /device:TPU:0, one launch (start us, length us, event | category | flops | bytes accessed | tf_op | source)
XLA Modules:
  0.0 107.8 jit_solution(5954510945601863834)
XLA Ops:
  3.5 3.0 %collective-permute-start = (bf16[3,1024]{1,0:T(4,128)(2,1)S(1)}, bf16[3,1024]{1,0:T(4,128)(2,1)S(1)}, u32[]{:S(2)}, u32[]{:S(2)}) collective-permute-start(bf16[3,1024]{1,0:T(4,128)(2,1)S(1)} %get-tuple-element.49), channel_id=1, source_target_pairs={{0,4},{4,8},{8,12},{12,16},{16,20},{20,24},{24,28},{1,5},{5,9},{9,... | collective-permute-start | bytes 18440 | tf_op jit(solution)/shard_map/ppermute | solution.py:10
  10.0 1.6 %add_multiply_fusion = f32[256,1024]{1,0:T(8,128)S(1)} fusion(f32[259,1024]{1,0:T(8,128)S(1)} %maximum_convert_fusion, bf16[256,1024]{1,0:T(8,128)(2,1)S(1)} %copy-done.4, f32[1024]{0:T(1024)S(1)} %bitcast.18, f32[1024]{0:T(1024)S(1)} %bitcast.21, f32[1024]{0:T(1024)S(1)} %bitcast.15, f32[1024]{0:T(1024)} %param.12, f32[1024]{0:T(1024)S(1)} %bitcast.12), kind=kLoop, calls=%fused_computation.39 | loop fusion | flops 4456448 | bytes 5787648 | tf_op jit(solution)/shard_map/mul | solution.py:25
  12.9 3.5 %fusion.4 = bf16[256,2048]{1,0:T(8,128)(2,1)S(1)} fusion(bf16[256,1024]{1,0:T(8,128)(2,1)S(1)} %fusion.16, bf16[4096,1024]{1,0:T(8,128)(2,1)} %param.9), kind=kOutput, calls=%fused_computation.4 | convolution fusion | flops 1074266112 | bytes 5767168 | tf_op jit(solution)/shard_map/dot_general | solution.py:105
  17.3 6.5 %collective-permute-start.2 = (bf16[64,2048]{1,0:T(8,128)(2,1)}, bf16[64,2048]{1,0:T(8,128)(2,1)}, u32[]{:S(2)}, u32[]{:S(2)}) collective-permute-start(bf16[64,2048]{1,0:T(8,128)(2,1)} %get-tuple-element.44), channel_id=1, source_target_pairs={{0,1},{3,2},{4,5},{7,6},{8,9},{11,10},{12,13},{15,14},{16,17},{19,... | collective-permute-start | bytes 786440 | tf_op jit(solution)/shard_map/ppermute | solution.py:63
  23.8 4.7 %fusion.7 = bf16[256,2048]{1,0:T(8,128)(2,1)} fusion(bf16[256,1024]{1,0:T(8,128)(2,1)} %copy-done.5, bf16[4096,1024]{1,0:T(8,128)(2,1)} %param.9), kind=kOutput, calls=%fused_computation.5 | convolution fusion | flops 1074266112 | bytes 5767168 | tf_op jit(solution)/shard_map/dot_general | solution.py:105
  28.5 2.0 %collective-permute-start.5 = (bf16[64,2048]{1,0:T(8,128)(2,1)}, bf16[64,2048]{1,0:T(8,128)(2,1)}, u32[]{:S(2)}, u32[]{:S(2)}) collective-permute-start(bf16[64,2048]{1,0:T(8,128)(2,1)} %get-tuple-element.43), channel_id=1, source_target_pairs={{0,1},{3,2},{4,5},{7,6},{8,9},{11,10},{12,13},{15,14},{16,17},{19,... | collective-permute-start | bytes 786440 | tf_op jit(solution)/shard_map/ppermute | solution.py:63
  30.5 2.0 %constant_dynamic-slice_fusion = (bf16[64,2048]{1,0:T(8,128)(2,1)S(1)}, bf16[64,2048]{1,0:T(8,128)(2,1)}, bf16[64,2048]{1,0:T(8,128)(2,1)}) fusion(bf16[256,2048]{1,0:T(8,128)(2,1)} %fusion.7, s32[]{:T(128)S(6)} %select_n.104, s32[]{:T(128)S(6)} %select_n.100, s32[]{:T(128)S(6)} %select_n.96), kind=kLoop, calls=%fused_computation.71 | loop fusion | bytes 1572876 | tf_op jit(solution)/shard_map/dynamic_slice | solution.py:46
  32.4 2.1 %collective-permute-start.7 = (bf16[64,2048]{1,0:T(8,128)(2,1)}, bf16[64,2048]{1,0:T(8,128)(2,1)}, u32[]{:S(2)}, u32[]{:S(2)}) collective-permute-start(bf16[64,2048]{1,0:T(8,128)(2,1)} %get-tuple-element.41), channel_id=1, source_target_pairs={{0,1},{3,2},{4,5},{7,6},{8,9},{11,10},{12,13},{15,14},{16,17},{19,... | collective-permute-start | bytes 786440 | tf_op jit(solution)/shard_map/ppermute | solution.py:63
  34.6 2.0 %collective-permute-start.10 = (bf16[64,2048]{1,0:T(8,128)(2,1)}, bf16[64,2048]{1,0:T(8,128)(2,1)}, u32[]{:S(2)}, u32[]{:S(2)}) collective-permute-start(bf16[64,2048]{1,0:T(8,128)(2,1)} %get-tuple-element.40), channel_id=1, source_target_pairs={{0,1},{3,2},{4,5},{7,6},{8,9},{11,10},{12,13},{15,14},{16,17},{19,... | collective-permute-start | bytes 786440 | tf_op jit(solution)/shard_map/ppermute | solution.py:63
  37.9 1.8 %add_convert_fusion.5 = bf16[64,2048]{1,0:T(8,128)(2,1)} fusion(bf16[64,2048]{1,0:T(8,128)(2,1)} %collective-permute-done.2, bf16[256,2048]{1,0:T(8,128)(2,1)} %copy-done.3, s32[]{:T(128)S(6)} %select_n.83), kind=kLoop, calls=%fused_computation.58 | loop fusion | flops 524288 | bytes 786436 | tf_op jit(solution)/shard_map/convert_element_type | solution.py:60
  39.7 1.8 %collective-permute-done.7 = bf16[64,2048]{1,0:T(8,128)(2,1)} collective-permute-done((bf16[64,2048]{1,0:T(8,128)(2,1)}, bf16[64,2048]{1,0:T(8,128)(2,1)}, u32[]{:S(2)}, u32[]{:S(2)}) %collective-permute-start.7) | collective-permute-done | bytes 262176 | tf_op jit(solution)/shard_map/ppermute | solution.py:63
  41.4 5.1 %collective-permute-start.17 = (bf16[64,2048]{1,0:T(8,128)(2,1)S(1)}, bf16[64,2048]{1,0:T(8,128)(2,1)}, u32[]{:S(2)}, u32[]{:S(2)}) collective-permute-start(bf16[64,2048]{1,0:T(8,128)(2,1)S(1)} %get-tuple-element.39), channel_id=1, source_target_pairs={{0,1},{3,2},{4,5},{7,6},{8,9},{11,10},{12,13},{15,14},{16,17},{19,... | collective-permute-start | bytes 786440 | tf_op jit(solution)/shard_map/ppermute | solution.py:63
  46.5 1.8 %add_convert_fusion.2 = bf16[64,2048]{1,0:T(8,128)(2,1)} fusion(bf16[64,2048]{1,0:T(8,128)(2,1)} %collective-permute-done.7, bf16[256,2048]{1,0:T(8,128)(2,1)} %fusion.7, s32[]{:T(128)S(6)} %select_n.94), kind=kLoop, calls=%fused_computation.54 | loop fusion | flops 524288 | bytes 786436 | tf_op jit(solution)/shard_map/convert_element_type | solution.py:60
  48.4 1.4 %collective-permute-start.3 = (bf16[64,2048]{1,0:T(8,128)(2,1)}, bf16[64,2048]{1,0:T(8,128)(2,1)}, u32[]{:S(2)}, u32[]{:S(2)}) collective-permute-start(bf16[64,2048]{1,0:T(8,128)(2,1)} %add_convert_fusion.5), channel_id=1, source_target_pairs={{1,2},{2,1},{5,6},{6,5},{9,10},{10,9},{13,14},{14,13},{17,18},{18,... | collective-permute-start | bytes 786440 | tf_op jit(solution)/shard_map/ppermute | solution.py:63
  51.0 2.2 %convert_divide_fusion = f32[64,4096]{1,0:T(8,128)} fusion(bf16[64,4096]{1,0:T(8,128)(2,1)} %collective-permute-done.12, f32[64]{0:T(128)S(1)} %add_sqrt_fusion), kind=kLoop, calls=%fused_computation.8 | loop fusion | flops 524288 | bytes 1573120 | tf_op jit(solution)/shard_map/div | solution.py:134
  55.8 1.7 %collective-permute-start.20 = (f32[5,1024]{1,0:T(8,128)S(1)}, f32[5,1024]{1,0:T(8,128)S(1)}, u32[]{:S(2)}, u32[]{:S(2)}) collective-permute-start(f32[5,1024]{1,0:T(8,128)S(1)} %stack.23), channel_id=1, source_target_pairs={{0,4},{4,0},{8,12},{12,8},{16,20},{20,16},{24,28},{28,24},{1,5},{5... | collective-permute-start | bytes 61448 | tf_op jit(solution)/shard_map/ppermute | solution.py:34
  59.6 1.4 %collective-permute-start.4 = (bf16[64,2048]{1,0:T(8,128)(2,1)S(1)}, bf16[64,2048]{1,0:T(8,128)(2,1)S(1)}, u32[]{:S(2)}, u32[]{:S(2)}) collective-permute-start(bf16[64,2048]{1,0:T(8,128)(2,1)S(1)} %get-tuple-element.47), channel_id=1, source_target_pairs={{2,3},{1,0},{6,7},{5,4},{10,11},{9,8},{14,15},{13,12},{18,19},{17,... | collective-permute-start | bytes 786440 | tf_op jit(solution)/shard_map/ppermute | solution.py:63
  63.0 12.9 %collective-permute-done.4 = bf16[64,2048]{1,0:T(8,128)(2,1)S(1)} collective-permute-done((bf16[64,2048]{1,0:T(8,128)(2,1)S(1)}, bf16[64,2048]{1,0:T(8,128)(2,1)S(1)}, u32[]{:S(2)}, u32[]{:S(2)}) %collective-permute-start.4) | collective-permute-done | bytes 262176 | tf_op jit(solution)/shard_map/ppermute | solution.py:63
  78.3 5.9 %collective-permute-done.9 = bf16[64,2048]{1,0:T(8,128)(2,1)S(1)} collective-permute-done((bf16[64,2048]{1,0:T(8,128)(2,1)S(1)}, bf16[64,2048]{1,0:T(8,128)(2,1)S(1)}, u32[]{:S(2)}, u32[]{:S(2)}) %collective-permute-start.9) | collective-permute-done | bytes 262176 | tf_op jit(solution)/shard_map/ppermute | solution.py:63
  85.8 5.4 %collective-permute-start.21 = (f32[5,1024]{1,0:T(8,128)S(1)}, f32[5,1024]{1,0:T(8,128)S(1)}, u32[]{:S(2)}, u32[]{:S(2)}) collective-permute-start(f32[5,1024]{1,0:T(8,128)S(1)} %add.231), channel_id=1, source_target_pairs={{0,8},{4,12},{8,0},{12,4},{16,24},{20,28},{24,16},{28,20},{1,9},{5... | collective-permute-start | bytes 61448 | tf_op jit(solution)/shard_map/ppermute | solution.py:34
  93.2 1.8 %collective-permute-done.14 = f32[4096]{0:T(1024)S(1)} collective-permute-done((f32[4096]{0:T(1024)S(1)}, f32[4096]{0:T(1024)S(1)}, u32[]{:S(2)}, u32[]{:S(2)}) %collective-permute-start.14) | collective-permute-done | bytes 16416 | tf_op jit(solution)/shard_map/ppermute | solution.py:34
  95.3 1.8 %collective-permute-done.22 = f32[5,1024]{1,0:T(8,128)S(1)} collective-permute-done((f32[5,1024]{1,0:T(8,128)S(1)}, f32[5,1024]{1,0:T(8,128)S(1)}, u32[]{:S(2)}, u32[]{:S(2)}) %collective-permute-start.22) | collective-permute-done | bytes 20512 | tf_op jit(solution)/shard_map/ppermute | solution.py:34
  100.2 2.3 %collective-permute-done.18 = f32[4096]{0:T(1024)S(1)} collective-permute-done((f32[4096]{0:T(1024)S(1)}, f32[4096]{0:T(1024)S(1)}, u32[]{:S(2)}, u32[]{:S(2)}) %collective-permute-start.18) | collective-permute-done | bytes 16416 | tf_op jit(solution)/shard_map/ppermute | solution.py:34
  103.6 3.6 %collective-permute-done.19 = f32[4096]{0:T(1024)S(1)} collective-permute-done((f32[4096]{0:T(1024)S(1)}, f32[4096]{0:T(1024)S(1)}, u32[]{:S(2)}, u32[]{:S(2)}) %collective-permute-start.19) | collective-permute-done | bytes 16416 | tf_op jit(solution)/shard_map/ppermute | solution.py:34
  (82 shorter events, 28.6 us)
Async XLA Ops:
  2.2 9.3 %collective-permute-start.1 = (bf16[6,1024]{1,0:T(8,128)(2,1)S(1)}, bf16[6,1024]{1,0:T(8,128)(2,1)S(1)}, u32[]{:S(2)}, u32[]{:S(2)}) collective-permute-start(bf16[6,1024]{1,0:T(8,128)(2,1)S(1)} %pad_maximum_fusion.1), channel_id=1, source_target_pairs={{4,0},{8,4},{12,8},{16,12},{20,16},{24,20},{28,24},{5,1},{9,5},{13... | collective-permute-start | bytes 36872 | tf_op jit(solution)/shard_map/ppermute | solution.py:10
  3.5 5.2 %collective-permute-start = (bf16[3,1024]{1,0:T(4,128)(2,1)S(1)}, bf16[3,1024]{1,0:T(4,128)(2,1)S(1)}, u32[]{:S(2)}, u32[]{:S(2)}) collective-permute-start(bf16[3,1024]{1,0:T(4,128)(2,1)S(1)} %get-tuple-element.49), channel_id=1, source_target_pairs={{0,4},{4,8},{8,12},{12,16},{16,20},{20,24},{24,28},{1,5},{5,9},{9,... | collective-permute-start | bytes 18440 | tf_op jit(solution)/shard_map/ppermute | solution.py:10
  6.5 41.8 %collective-permute-start.12 = (bf16[64,4096]{1,0:T(8,128)(2,1)}, bf16[64,4096]{1,0:T(8,128)(2,1)}, u32[]{:S(2)}, u32[]{:S(2)}) collective-permute-start(bf16[64,4096]{1,0:T(8,128)(2,1)} %param.7), channel_id=1, source_target_pairs={{1,0},{2,3},{5,4},{6,7},{9,8},{10,11},{13,12},{14,15},{17,16},{18,... | collective-permute-start | bytes 1572872 | tf_op jit(solution)/shard_map/ppermute | solution.py:85
  17.3 19.2 %collective-permute-start.2 = (bf16[64,2048]{1,0:T(8,128)(2,1)}, bf16[64,2048]{1,0:T(8,128)(2,1)}, u32[]{:S(2)}, u32[]{:S(2)}) collective-permute-start(bf16[64,2048]{1,0:T(8,128)(2,1)} %get-tuple-element.44), channel_id=1, source_target_pairs={{0,1},{3,2},{4,5},{7,6},{8,9},{11,10},{12,13},{15,14},{16,17},{19,... | collective-permute-start | bytes 786440 | tf_op jit(solution)/shard_map/ppermute | solution.py:63
  28.5 26.7 %collective-permute-start.5 = (bf16[64,2048]{1,0:T(8,128)(2,1)}, bf16[64,2048]{1,0:T(8,128)(2,1)}, u32[]{:S(2)}, u32[]{:S(2)}) collective-permute-start(bf16[64,2048]{1,0:T(8,128)(2,1)} %get-tuple-element.43), channel_id=1, source_target_pairs={{0,1},{3,2},{4,5},{7,6},{8,9},{11,10},{12,13},{15,14},{16,17},{19,... | collective-permute-start | bytes 786440 | tf_op jit(solution)/shard_map/ppermute | solution.py:63
  32.4 9.0 %collective-permute-start.7 = (bf16[64,2048]{1,0:T(8,128)(2,1)}, bf16[64,2048]{1,0:T(8,128)(2,1)}, u32[]{:S(2)}, u32[]{:S(2)}) collective-permute-start(bf16[64,2048]{1,0:T(8,128)(2,1)} %get-tuple-element.41), channel_id=1, source_target_pairs={{0,1},{3,2},{4,5},{7,6},{8,9},{11,10},{12,13},{15,14},{16,17},{19,... | collective-permute-start | bytes 786440 | tf_op jit(solution)/shard_map/ppermute | solution.py:63
  34.6 24.3 %collective-permute-start.10 = (bf16[64,2048]{1,0:T(8,128)(2,1)}, bf16[64,2048]{1,0:T(8,128)(2,1)}, u32[]{:S(2)}, u32[]{:S(2)}) collective-permute-start(bf16[64,2048]{1,0:T(8,128)(2,1)} %get-tuple-element.40), channel_id=1, source_target_pairs={{0,1},{3,2},{4,5},{7,6},{8,9},{11,10},{12,13},{15,14},{16,17},{19,... | collective-permute-start | bytes 786440 | tf_op jit(solution)/shard_map/ppermute | solution.py:63
  36.6 62.1 %collective-permute-start.16 = (bf16[64,2048]{1,0:T(8,128)(2,1)S(1)}, bf16[64,2048]{1,0:T(8,128)(2,1)S(1)}, u32[]{:S(2)}, u32[]{:S(2)}) collective-permute-start(bf16[64,2048]{1,0:T(8,128)(2,1)S(1)} %get-tuple-element.42), channel_id=1, source_target_pairs={{0,1},{3,2},{4,5},{7,6},{8,9},{11,10},{12,13},{15,14},{16,17},{19,... | collective-permute-start | bytes 786440 | tf_op jit(solution)/shard_map/ppermute | solution.py:63
  41.4 57.3 %collective-permute-start.17 = (bf16[64,2048]{1,0:T(8,128)(2,1)S(1)}, bf16[64,2048]{1,0:T(8,128)(2,1)}, u32[]{:S(2)}, u32[]{:S(2)}) collective-permute-start(bf16[64,2048]{1,0:T(8,128)(2,1)S(1)} %get-tuple-element.39), channel_id=1, source_target_pairs={{0,1},{3,2},{4,5},{7,6},{8,9},{11,10},{12,13},{15,14},{16,17},{19,... | collective-permute-start | bytes 786440 | tf_op jit(solution)/shard_map/ppermute | solution.py:63
  48.4 7.5 %collective-permute-start.3 = (bf16[64,2048]{1,0:T(8,128)(2,1)}, bf16[64,2048]{1,0:T(8,128)(2,1)}, u32[]{:S(2)}, u32[]{:S(2)}) collective-permute-start(bf16[64,2048]{1,0:T(8,128)(2,1)} %add_convert_fusion.5), channel_id=1, source_target_pairs={{1,2},{2,1},{5,6},{6,5},{9,10},{10,9},{13,14},{14,13},{17,18},{18,... | collective-permute-start | bytes 786440 | tf_op jit(solution)/shard_map/ppermute | solution.py:63
  55.1 4.5 %collective-permute-start.8 = (bf16[64,2048]{1,0:T(8,128)(2,1)}, bf16[64,2048]{1,0:T(8,128)(2,1)S(1)}, u32[]{:S(2)}, u32[]{:S(2)}) collective-permute-start(bf16[64,2048]{1,0:T(8,128)(2,1)} %add_convert_fusion.2), channel_id=1, source_target_pairs={{1,2},{2,1},{5,6},{6,5},{9,10},{10,9},{13,14},{14,13},{17,18},{18,... | collective-permute-start | bytes 786440 | tf_op jit(solution)/shard_map/ppermute | solution.py:63
  55.8 29.9 %collective-permute-start.20 = (f32[5,1024]{1,0:T(8,128)S(1)}, f32[5,1024]{1,0:T(8,128)S(1)}, u32[]{:S(2)}, u32[]{:S(2)}) collective-permute-start(f32[5,1024]{1,0:T(8,128)S(1)} %stack.23), channel_id=1, source_target_pairs={{0,4},{4,0},{8,12},{12,8},{16,20},{20,16},{24,28},{28,24},{1,5},{5... | collective-permute-start | bytes 61448 | tf_op jit(solution)/shard_map/ppermute | solution.py:34
  58.9 3.4 %collective-permute-start.6 = (bf16[64,2048]{1,0:T(8,128)(2,1)S(1)}, bf16[64,2048]{1,0:T(8,128)(2,1)S(1)}, u32[]{:S(2)}, u32[]{:S(2)}) collective-permute-start(bf16[64,2048]{1,0:T(8,128)(2,1)S(1)} %get-tuple-element.48), channel_id=1, source_target_pairs={{1,2},{2,1},{5,6},{6,5},{9,10},{10,9},{13,14},{14,13},{17,18},{18,... | collective-permute-start | bytes 786440 | tf_op jit(solution)/shard_map/ppermute | solution.py:63
  59.6 25.6 %copy-start.1 = (f32[64,4096]{1,0:T(8,128)S(1)}, f32[64,4096]{1,0:T(8,128)}, u32[]{:S(2)}) copy-start(f32[64,4096]{1,0:T(8,128)} %convert_divide_fusion) | copy-start | bytes 3145732
  59.6 16.3 %collective-permute-start.4 = (bf16[64,2048]{1,0:T(8,128)(2,1)S(1)}, bf16[64,2048]{1,0:T(8,128)(2,1)S(1)}, u32[]{:S(2)}, u32[]{:S(2)}) collective-permute-start(bf16[64,2048]{1,0:T(8,128)(2,1)S(1)} %get-tuple-element.47), channel_id=1, source_target_pairs={{2,3},{1,0},{6,7},{5,4},{10,11},{9,8},{14,15},{13,12},{18,19},{17,... | collective-permute-start | bytes 786440 | tf_op jit(solution)/shard_map/ppermute | solution.py:63
  62.3 16.0 %collective-permute-start.11 = (bf16[64,2048]{1,0:T(8,128)(2,1)S(1)}, bf16[64,2048]{1,0:T(8,128)(2,1)S(1)}, u32[]{:S(2)}, u32[]{:S(2)}) collective-permute-start(bf16[64,2048]{1,0:T(8,128)(2,1)S(1)} %get-tuple-element.46), channel_id=1, source_target_pairs={{1,2},{2,1},{5,6},{6,5},{9,10},{10,9},{13,14},{14,13},{17,18},{18,... | collective-permute-start | bytes 786440 | tf_op jit(solution)/shard_map/ppermute | solution.py:63
  75.9 8.3 %collective-permute-start.9 = (bf16[64,2048]{1,0:T(8,128)(2,1)S(1)}, bf16[64,2048]{1,0:T(8,128)(2,1)S(1)}, u32[]{:S(2)}, u32[]{:S(2)}) collective-permute-start(bf16[64,2048]{1,0:T(8,128)(2,1)S(1)} %get-tuple-element.45), channel_id=1, source_target_pairs={{2,3},{1,0},{6,7},{5,4},{10,11},{9,8},{14,15},{13,12},{18,19},{17,... | collective-permute-start | bytes 786440 | tf_op jit(solution)/shard_map/ppermute | solution.py:63
  85.7 5.5 %collective-permute-start.13 = (f32[4096]{0:T(1024)S(1)}, f32[4096]{0:T(1024)S(1)}, u32[]{:S(2)}, u32[]{:S(2)}) collective-permute-start(f32[4096]{0:T(1024)S(1)} %pad_maximum_fusion.2), channel_id=1, source_target_pairs={{0,4},{4,0},{8,12},{12,8},{16,20},{20,16},{24,28},{28,24},{1,5},{5... | collective-permute-start | bytes 49160 | tf_op jit(solution)/shard_map/ppermute | solution.py:34
  85.8 7.4 %collective-permute-start.21 = (f32[5,1024]{1,0:T(8,128)S(1)}, f32[5,1024]{1,0:T(8,128)S(1)}, u32[]{:S(2)}, u32[]{:S(2)}) collective-permute-start(f32[5,1024]{1,0:T(8,128)S(1)} %add.231), channel_id=1, source_target_pairs={{0,8},{4,12},{8,0},{12,4},{16,24},{20,28},{24,16},{28,20},{1,9},{5... | collective-permute-start | bytes 61448 | tf_op jit(solution)/shard_map/ppermute | solution.py:34
  91.2 3.8 %collective-permute-start.14 = (f32[4096]{0:T(1024)S(1)}, f32[4096]{0:T(1024)S(1)}, u32[]{:S(2)}, u32[]{:S(2)}) collective-permute-start(f32[4096]{0:T(1024)S(1)} %add.224), channel_id=1, source_target_pairs={{0,8},{4,12},{8,0},{12,4},{16,24},{20,28},{24,16},{28,20},{1,9},{5... | collective-permute-start | bytes 49160 | tf_op jit(solution)/shard_map/ppermute | solution.py:34
  93.2 3.9 %collective-permute-start.22 = (f32[5,1024]{1,0:T(8,128)S(1)}, f32[5,1024]{1,0:T(8,128)S(1)}, u32[]{:S(2)}, u32[]{:S(2)}) collective-permute-start(f32[5,1024]{1,0:T(8,128)S(1)} %add.232), channel_id=1, source_target_pairs={{0,16},{4,20},{8,24},{12,28},{16,0},{20,4},{24,8},{28,12},{1,17},{... | collective-permute-start | bytes 61448 | tf_op jit(solution)/shard_map/ppermute | solution.py:34
  95.0 3.7 %collective-permute-start.15 = (f32[4096]{0:T(1024)S(1)}, f32[4096]{0:T(1024)S(1)}, u32[]{:S(2)}, u32[]{:S(2)}) collective-permute-start(f32[4096]{0:T(1024)S(1)} %add.225), channel_id=1, source_target_pairs={{0,16},{4,20},{8,24},{12,28},{16,0},{20,4},{24,8},{28,12},{1,17},{... | collective-permute-start | bytes 49160 | tf_op jit(solution)/shard_map/ppermute | solution.py:34
  98.7 3.8 %collective-permute-start.18 = (f32[4096]{0:T(1024)S(1)}, f32[4096]{0:T(1024)S(1)}, u32[]{:S(2)}, u32[]{:S(2)}) collective-permute-start(f32[4096]{0:T(1024)S(1)} %add.226), channel_id=1, source_target_pairs={{0,1},{1,0},{2,3},{3,2},{4,5},{5,4},{6,7},{7,6},{8,9},{9,8},{10,11... | collective-permute-start | bytes 49160 | tf_op jit(solution)/shard_map/ppermute | solution.py:34
  102.5 4.6 %collective-permute-start.19 = (f32[4096]{0:T(1024)S(1)}, f32[4096]{0:T(1024)S(1)}, u32[]{:S(2)}, u32[]{:S(2)}) collective-permute-start(f32[4096]{0:T(1024)S(1)} %add.229), channel_id=1, source_target_pairs={{0,2},{1,3},{2,0},{3,1},{4,6},{5,7},{6,4},{7,5},{8,10},{9,11},{10,... | collective-permute-start | bytes 49160 | tf_op jit(solution)/shard_map/ppermute | solution.py:34
  (7 other events, 84.4 us)

commit v4 on v1

--- a/solution.py
+++ b/solution.py
@@ -31,7 +31,8 @@
         return lax.psum(value, axis)
     step = 1
     while step < size:
-        value = value + lax.ppermute(value, axis, [(i, i ^ step) for i in range(size)])
+        arrived = lax.ppermute(value, axis, [(i, i ^ step) for i in range(size)])
+        value = value + arrived
         step *= 2
     return value
 
@@ -53,10 +54,11 @@
     for hop in range(1, size):
         send_right = joined(block(size - hop + place), right)
         send_left = joined(block(hop - size + place), left)
+        send_right, send_left = lax.optimization_barrier((send_right, send_left))
         right = lax.ppermute(send_right, axis, [(i, i + 1) for i in range(hop)])
         left = lax.ppermute(send_left, axis, [(size - 1 - i, size - 2 - i) for i in range(hop)])
         if hop < size - 1:
-            yield None
+            yield right
     total = block(place).astype(jnp.float32)
     if right is not None:
         total = total + right.astype(jnp.float32) + left.astype(jnp.float32)
@@ -86,7 +88,7 @@
             for index in range(tap_count)
         )
     ).astype(jnp.bfloat16)
-    in_grad = lax.optimization_barrier(in_grad)
+    in_grad, pre_grad, padded = lax.optimization_barrier((in_grad, pre_grad, padded))
     width = proj_weight.shape[0]
     chunk = width // CHUNKS
     streams = []
@@ -99,9 +101,12 @@
         ).astype(jnp.bfloat16)
         streams.append(line_scatter_parts(lax.optimization_barrier(part), "tp"))
     sums = [None] * CHUNKS
+    first = None
     for _ in range(max(lax.axis_size("tp") - 1, 1)):
         for index in range(CHUNKS):
             sums[index] = next(streams[index])
+            first = sums[index] if first is None else first
+    pre_grad, padded, hidden_in, _ = lax.optimization_barrier((pre_grad, padded, hidden_in, first))
     taps_part = jnp.stack(
         [
             jnp.sum(pre_grad * padded[edge_rows - index : edge_rows - index + count_tok], 0)

time: 87.2 us -> 86 us (0.986)
  waiting for transfers between devices: 21.1 us -> 16.9 us
  matrix products: 6.95 us -> 4.91 us
  other arithmetic: 7.13 us -> 9.17 us
  starting transfers between devices: 46.5 us -> 48.5 us
  local copies, waits for them, and re-layouts: 3.79 us -> 4.71 us
    ppermute x6, waiting for transfers between devices: 11.2 us -> 5.1 us  [line_scatter_parts(): lax.ppermute(send_left, axis, [(size - 1 - i, size - 2 - i) for i in rang...]
    ppermute x8, starting transfers between devices: 14 us -> 10.3 us  [xor_sum(): arrived = lax.ppermute(value, axis, [(i, i ^ step) for i in range(size)])]
    ppermute x6, starting transfers between devices: 23.5 us -> 27.2 us  [line_scatter_parts(): right = lax.ppermute(send_right, axis, [(i, i + 1) for i in range(hop)])]
    convert_element_type x6 -> x4, other arithmetic: 0.54 us -> 2.66 us  [joined(): (own.astype(jnp.float32) + arrived.astype(jnp.float32)).astype(part.dtype)]
    dot_general x2, matrix products: 6.95 us -> 4.91 us  [on_device(): lax.dot_general(in_grad, proj_weight[index * chunk:(index + 1) * chunk],...]
    mul x1 -> x2, other arithmetic: 0.05 us -> 1.71 us  [grad_of(): cotangent.astype(jnp.float32) * sigmoid_v]
    ppermute x6, starting transfers between devices: 5.29 us -> 6.71 us  [line_scatter_parts(): lax.ppermute(send_left, axis, [(size - 1 - i, size - 2 - i) for i in rang...]
    ppermute x8, waiting for transfers between devices: 6.74 us -> 7.81 us  [xor_sum(): arrived = lax.ppermute(value, axis, [(i, i ^ step) for i in range(size)])]
  transfers between devices with their start and end apart: 22 -> 22, of which waited for: 9 -> 9; matrix products, arithmetic and copies ran while one was open for 19% -> 12% of each run, Pallas kernels for 0% -> 0%
where the time goes in v4:
time: 86 us; the launch traced here: 85.3 us
  starting transfers between devices  48.5 us (56%)
  waiting for transfers between devices  16.9 us (20%)
  other arithmetic  9.17 us (11%)
  matrix products  4.91 us (6%)
  local copies, waits for them, and re-layouts  4.71 us (5%)
  between operations  1.09 us (1%)
    ppermute x6, starting transfers between devices, line_scatter_parts(): right = lax.ppermute(send_right, axis, [(i, i + 1) for i in range(hop)])  27.2 us
    ppermute x8, starting transfers between devices, xor_sum(): arrived = lax.ppermute(value, axis, [(i, i ^ step) for i in range(size)])  10.3 us
    ppermute x8, waiting for transfers between devices, xor_sum(): arrived = lax.ppermute(value, axis, [(i, i ^ step) for i in range(size)])  7.81 us
    ppermute x6, starting transfers between devices, line_scatter_parts(): lax.ppermute(send_left, axis, [(size - 1 - i, size - 2 - i) for i in rang...  6.71 us
    ppermute x6, waiting for transfers between devices, line_scatter_parts(): lax.ppermute(send_left, axis, [(size - 1 - i, size - 2 - i) for i in rang...  5.1 us
    dot_general x2, matrix products, on_device(): lax.dot_general(in_grad, proj_weight[index * chunk:(index + 1) * chunk],...  4.91 us
    ppermute x2, starting transfers between devices, from_behind(): return lax.ppermute(block, axis, route)  4.32 us
    ppermute x6, waiting for transfers between devices, line_scatter_parts(): right = lax.ppermute(send_right, axis, [(i, i + 1) for i in range(hop)])  3.97 us
  transfers between devices with their start and end apart: 22, of which 9 were waited for; matrix products, arithmetic and copies ran while one was open for 12% of the time, Pallas kernels for 0%

profile of v4, /device:TPU:0, one launch (start us, length us, event | category | flops | bytes accessed | tf_op | source)
XLA Modules:
  0.0 85.3 jit_solution(15027989318515124442)
XLA Ops:
  2.2 1.3 %collective-permute-start.1 = (bf16[6,1024]{1,0:T(8,128)(2,1)S(1)}, bf16[6,1024]{1,0:T(8,128)(2,1)S(1)}, u32[]{:S(2)}, u32[]{:S(2)}) collective-permute-start(bf16[6,1024]{1,0:T(8,128)(2,1)S(1)} %pad_maximum_fusion.2), channel_id=1, source_target_pairs={{4,0},{8,4},{12,8},{16,12},{20,16},{24,20},{28,24},{5,1},{9,5},{13... | collective-permute-start | bytes 36872 | tf_op jit(solution)/shard_map/ppermute | solution.py:10
  3.5 3.0 %collective-permute-start = (bf16[3,1024]{1,0:T(4,128)(2,1)S(1)}, bf16[3,1024]{1,0:T(4,128)(2,1)S(1)}, u32[]{:S(2)}, u32[]{:S(2)}) collective-permute-start(bf16[3,1024]{1,0:T(4,128)(2,1)S(1)} %get-tuple-element.59), channel_id=1, source_target_pairs={{0,4},{4,8},{8,12},{12,16},{16,20},{20,24},{24,28},{1,5},{5,9},{9,... | collective-permute-start | bytes 18440 | tf_op jit(solution)/shard_map/ppermute | solution.py:10
  8.7 1.7 %add_multiply_fusion = f32[256,1024]{1,0:T(8,128)S(1)} fusion(f32[259,1024]{1,0:T(8,128)S(1)} %maximum_convert_fusion, bf16[256,1024]{1,0:T(8,128)(2,1)S(1)} %copy-done.3, f32[1024]{0:T(1024)S(1)} %bitcast.18, f32[1024]{0:T(1024)S(1)} %bitcast.21, f32[1024]{0:T(1024)S(1)} %bitcast.15, f32[1024]{0:T(1024)} %param.12, f32[1024]{0:T(1024)S(1)} %bitcast.12), kind=kLoop, calls=%fused_computation.37 | loop fusion | flops 4456448 | bytes 5787648 | tf_op jit(solution)/shard_map/mul | solution.py:25
  10.9 3.6 %fusion.4 = bf16[256,2048]{1,0:T(8,128)(2,1)S(1)} fusion(bf16[256,1024]{1,0:T(8,128)(2,1)S(1)} %fusion.15, bf16[4096,1024]{1,0:T(8,128)(2,1)} %param.9), kind=kOutput, calls=%fused_computation.4 | convolution fusion | flops 1074266112 | bytes 5767168 | tf_op jit(solution)/shard_map/dot_general | solution.py:96
  14.6 1.3 %fusion.7 = bf16[256,2048]{1,0:T(8,128)(2,1)S(1)} fusion(bf16[256,1024]{1,0:T(8,128)(2,1)S(1)} %fusion.15, bf16[4096,1024]{1,0:T(8,128)(2,1)S(1)} %bitcast.31), kind=kOutput, calls=%fused_computation.5 | convolution fusion | flops 1074266112 | bytes 5767168 | tf_op jit(solution)/shard_map/dot_general | solution.py:96
  16.9 5.0 %collective-permute-start.2 = (bf16[64,2048]{1,0:T(8,128)(2,1)}, bf16[64,2048]{1,0:T(8,128)(2,1)S(1)}, u32[]{:S(2)}, u32[]{:S(2)}) collective-permute-start(bf16[64,2048]{1,0:T(8,128)(2,1)} %get-tuple-element.23), channel_id=1, source_target_pairs={{0,1},{4,5},{8,9},{12,13},{16,17},{20,21},{24,25},{28,29}} | collective-permute-start | bytes 786440 | tf_op jit(solution)/shard_map/ppermute | solution.py:58
  21.9 1.4 %collective-permute-start.3 = (bf16[64,2048]{1,0:T(8,128)(2,1)}, bf16[64,2048]{1,0:T(8,128)(2,1)}, u32[]{:S(2)}, u32[]{:S(2)}) collective-permute-start(bf16[64,2048]{1,0:T(8,128)(2,1)} %get-tuple-element.24), channel_id=1, source_target_pairs={{3,2},{7,6},{11,10},{15,14},{19,18},{23,22},{27,26},{31,30}} | collective-permute-start | bytes 786440 | tf_op jit(solution)/shard_map/ppermute | solution.py:59
  23.3 2.0 %collective-permute-start.8 = (bf16[64,2048]{1,0:T(8,128)(2,1)}, bf16[64,2048]{1,0:T(8,128)(2,1)}, u32[]{:S(2)}, u32[]{:S(2)}) collective-permute-start(bf16[64,2048]{1,0:T(8,128)(2,1)} %get-tuple-element.29), channel_id=1, source_target_pairs={{0,1},{4,5},{8,9},{12,13},{16,17},{20,21},{24,25},{28,29}} | collective-permute-start | bytes 786440 | tf_op jit(solution)/shard_map/ppermute | solution.py:58
  25.3 1.4 %collective-permute-start.9 = (bf16[64,2048]{1,0:T(8,128)(2,1)}, bf16[64,2048]{1,0:T(8,128)(2,1)}, u32[]{:S(2)}, u32[]{:S(2)}) collective-permute-start(bf16[64,2048]{1,0:T(8,128)(2,1)} %get-tuple-element.30), channel_id=1, source_target_pairs={{3,2},{7,6},{11,10},{15,14},{19,18},{23,22},{27,26},{31,30}} | collective-permute-start | bytes 786440 | tf_op jit(solution)/shard_map/ppermute | solution.py:59
  26.6 2.1 %collective-permute-done.2 = bf16[64,2048]{1,0:T(8,128)(2,1)S(1)} collective-permute-done((bf16[64,2048]{1,0:T(8,128)(2,1)}, bf16[64,2048]{1,0:T(8,128)(2,1)S(1)}, u32[]{:S(2)}, u32[]{:S(2)}) %collective-permute-start.2) | collective-permute-done | bytes 262176 | tf_op jit(solution)/shard_map/ppermute | solution.py:58
  29.8 1.2 %add_convert_fusion.6 = (bf16[64,2048]{1,0:T(8,128)(2,1)S(1)}, bf16[64,2048]{1,0:T(8,128)(2,1)S(1)}) fusion(bf16[64,2048]{1,0:T(8,128)(2,1)} %collective-permute-done.3, bf16[256,2048]{1,0:T(8,128)(2,1)} %copy-done.1, s32[]{:T(128)S(6)} %select_n.33, bf16[64,2048]{1,0:T(8,128)(2,1)S(1)} %collective-permute-done.2, s32[]{:T(128)S(6)} %select_n.30), kind=kLoop, calls=%fused_computation.47 | loop fusion | flops 1048576 | bytes 1572872 | tf_op jit(solution)/shard_map/convert_element_type | solution.py:51
  31.0 4.4 %collective-permute-start.4 = (bf16[64,2048]{1,0:T(8,128)(2,1)S(1)}, bf16[64,2048]{1,0:T(8,128)(2,1)S(1)}, u32[]{:S(2)}, u32[]{:S(2)}) collective-permute-start(bf16[64,2048]{1,0:T(8,128)(2,1)S(1)} %get-tuple-element.25), channel_id=1, source_target_pairs={{0,1},{1,2},{4,5},{5,6},{8,9},{9,10},{12,13},{13,14},{16,17},{17,1... | collective-permute-start | bytes 786440 | tf_op jit(solution)/shard_map/ppermute | solution.py:58
  37.5 3.7 %collective-permute-start.10 = (bf16[64,2048]{1,0:T(8,128)(2,1)S(1)}, bf16[64,2048]{1,0:T(8,128)(2,1)S(1)}, u32[]{:S(2)}, u32[]{:S(2)}) collective-permute-start(bf16[64,2048]{1,0:T(8,128)(2,1)S(1)} %get-tuple-element.31), channel_id=1, source_target_pairs={{0,1},{1,2},{4,5},{5,6},{8,9},{9,10},{12,13},{13,14},{16,17},{17,1... | collective-permute-start | bytes 786440 | tf_op jit(solution)/shard_map/ppermute | solution.py:58
  42.1 6.8 %collective-permute-start.6 = (bf16[64,2048]{1,0:T(8,128)(2,1)S(1)}, bf16[64,2048]{1,0:T(8,128)(2,1)S(1)}, u32[]{:S(2)}, u32[]{:S(2)}) collective-permute-start(bf16[64,2048]{1,0:T(8,128)(2,1)S(1)} %get-tuple-element.27), channel_id=1, source_target_pairs={{0,1},{1,2},{2,3},{4,5},{5,6},{6,7},{8,9},{9,10},{10,11},{12,13},{... | collective-permute-start | bytes 786440 | tf_op jit(solution)/shard_map/ppermute | solution.py:58
  48.9 1.3 %collective-permute-start.7 = (bf16[64,2048]{1,0:T(8,128)(2,1)S(1)}, bf16[64,2048]{1,0:T(8,128)(2,1)S(1)}, u32[]{:S(2)}, u32[]{:S(2)}) collective-permute-start(bf16[64,2048]{1,0:T(8,128)(2,1)S(1)} %get-tuple-element.28), channel_id=1, source_target_pairs={{3,2},{2,1},{1,0},{7,6},{6,5},{5,4},{11,10},{10,9},{9,8},{15,14},{... | collective-permute-start | bytes 786440 | tf_op jit(solution)/shard_map/ppermute | solution.py:59
  50.4 5.3 %collective-permute-start.12 = (bf16[64,2048]{1,0:T(8,128)(2,1)S(1)}, bf16[64,2048]{1,0:T(8,128)(2,1)S(1)}, u32[]{:S(2)}, u32[]{:S(2)}) collective-permute-start(bf16[64,2048]{1,0:T(8,128)(2,1)S(1)} %get-tuple-element.33), channel_id=1, source_target_pairs={{0,1},{1,2},{2,3},{4,5},{5,6},{6,7},{8,9},{9,10},{10,11},{12,13},{... | collective-permute-start | bytes 786440 | tf_op jit(solution)/shard_map/ppermute | solution.py:58
  55.7 1.3 %collective-permute-start.13 = (bf16[64,2048]{1,0:T(8,128)(2,1)S(1)}, bf16[64,2048]{1,0:T(8,128)(2,1)S(1)}, u32[]{:S(2)}, u32[]{:S(2)}) collective-permute-start(bf16[64,2048]{1,0:T(8,128)(2,1)S(1)} %get-tuple-element.34), channel_id=1, source_target_pairs={{3,2},{2,1},{1,0},{7,6},{6,5},{5,4},{11,10},{10,9},{9,8},{15,14},{... | collective-permute-start | bytes 786440 | tf_op jit(solution)/shard_map/ppermute | solution.py:59
  58.1 1.9 %collective-permute-done.12 = bf16[64,2048]{1,0:T(8,128)(2,1)S(1)} collective-permute-done((bf16[64,2048]{1,0:T(8,128)(2,1)S(1)}, bf16[64,2048]{1,0:T(8,128)(2,1)S(1)}, u32[]{:S(2)}, u32[]{:S(2)}) %collective-permute-start.12) | collective-permute-done | bytes 262176 | tf_op jit(solution)/shard_map/ppermute | solution.py:58
  60.0 4.1 %collective-permute-done.13 = bf16[64,2048]{1,0:T(8,128)(2,1)S(1)} collective-permute-done((bf16[64,2048]{1,0:T(8,128)(2,1)S(1)}, bf16[64,2048]{1,0:T(8,128)(2,1)S(1)}, u32[]{:S(2)}, u32[]{:S(2)}) %collective-permute-start.13) | collective-permute-done | bytes 262176 | tf_op jit(solution)/shard_map/ppermute | solution.py:59
  64.8 1.9 %collective-permute-start.20 = (f32[5,1024]{1,0:T(8,128)S(1)}, f32[5,1024]{1,0:T(8,128)S(1)}, u32[]{:S(2)}, u32[]{:S(2)}) collective-permute-start(f32[5,1024]{1,0:T(8,128)S(1)} %add.227), channel_id=1, source_target_pairs={{0,8},{4,12},{8,0},{12,4},{16,24},{20,28},{24,16},{28,20},{1,9},{5... | collective-permute-start | bytes 61448 | tf_op jit(solution)/shard_map/ppermute | solution.py:34
  68.8 3.7 %collective-permute-start.21 = (f32[5,1024]{1,0:T(8,128)S(1)}, f32[5,1024]{1,0:T(8,128)S(1)}, u32[]{:S(2)}, u32[]{:S(2)}) collective-permute-start(f32[5,1024]{1,0:T(8,128)S(1)} %add.228), channel_id=1, source_target_pairs={{0,16},{4,20},{8,24},{12,28},{16,0},{20,4},{24,8},{28,12},{1,17},{... | collective-permute-start | bytes 61448 | tf_op jit(solution)/shard_map/ppermute | solution.py:34
  76.3 1.4 %collective-permute-start.17 = (f32[4096]{0:T(1024)S(1)}, f32[4096]{0:T(1024)S(1)}, u32[]{:S(2)}, u32[]{:S(2)}) collective-permute-start(f32[4096]{0:T(1024)S(1)} %add.224), channel_id=1, source_target_pairs={{0,1},{1,0},{2,3},{3,2},{4,5},{5,4},{6,7},{7,6},{8,9},{9,8},{10,11... | collective-permute-start | bytes 49160 | tf_op jit(solution)/shard_map/ppermute | solution.py:34
  77.7 2.4 %collective-permute-done.17 = f32[4096]{0:T(1024)S(1)} collective-permute-done((f32[4096]{0:T(1024)S(1)}, f32[4096]{0:T(1024)S(1)}, u32[]{:S(2)}, u32[]{:S(2)}) %collective-permute-start.17) | collective-permute-done | bytes 16416 | tf_op jit(solution)/shard_map/ppermute | solution.py:34
  82.0 2.7 %collective-permute-done.18 = f32[4096]{0:T(1024)S(1)} collective-permute-done((f32[4096]{0:T(1024)S(1)}, f32[4096]{0:T(1024)S(1)}, u32[]{:S(2)}, u32[]{:S(2)}) %collective-permute-start.18) | collective-permute-done | bytes 16416 | tf_op jit(solution)/shard_map/ppermute | solution.py:34
  (73 shorter events, 19.3 us)
Async XLA Ops:
  2.2 8.1 %collective-permute-start.1 = (bf16[6,1024]{1,0:T(8,128)(2,1)S(1)}, bf16[6,1024]{1,0:T(8,128)(2,1)S(1)}, u32[]{:S(2)}, u32[]{:S(2)}) collective-permute-start(bf16[6,1024]{1,0:T(8,128)(2,1)S(1)} %pad_maximum_fusion.2), channel_id=1, source_target_pairs={{4,0},{8,4},{12,8},{16,12},{20,16},{24,20},{28,24},{5,1},{9,5},{13... | collective-permute-start | bytes 36872 | tf_op jit(solution)/shard_map/ppermute | solution.py:10
  3.5 3.9 %collective-permute-start = (bf16[3,1024]{1,0:T(4,128)(2,1)S(1)}, bf16[3,1024]{1,0:T(4,128)(2,1)S(1)}, u32[]{:S(2)}, u32[]{:S(2)}) collective-permute-start(bf16[3,1024]{1,0:T(4,128)(2,1)S(1)} %get-tuple-element.59), channel_id=1, source_target_pairs={{0,4},{4,8},{8,12},{12,16},{16,20},{20,24},{24,28},{1,5},{5,9},{9,... | collective-permute-start | bytes 18440 | tf_op jit(solution)/shard_map/ppermute | solution.py:10
  16.9 11.8 %collective-permute-start.2 = (bf16[64,2048]{1,0:T(8,128)(2,1)}, bf16[64,2048]{1,0:T(8,128)(2,1)S(1)}, u32[]{:S(2)}, u32[]{:S(2)}) collective-permute-start(bf16[64,2048]{1,0:T(8,128)(2,1)} %get-tuple-element.23), channel_id=1, source_target_pairs={{0,1},{4,5},{8,9},{12,13},{16,17},{20,21},{24,25},{28,29}} | collective-permute-start | bytes 786440 | tf_op jit(solution)/shard_map/ppermute | solution.py:58
  21.9 7.9 %collective-permute-start.3 = (bf16[64,2048]{1,0:T(8,128)(2,1)}, bf16[64,2048]{1,0:T(8,128)(2,1)}, u32[]{:S(2)}, u32[]{:S(2)}) collective-permute-start(bf16[64,2048]{1,0:T(8,128)(2,1)} %get-tuple-element.24), channel_id=1, source_target_pairs={{3,2},{7,6},{11,10},{15,14},{19,18},{23,22},{27,26},{31,30}} | collective-permute-start | bytes 786440 | tf_op jit(solution)/shard_map/ppermute | solution.py:59
  23.3 12.9 %collective-permute-start.8 = (bf16[64,2048]{1,0:T(8,128)(2,1)}, bf16[64,2048]{1,0:T(8,128)(2,1)}, u32[]{:S(2)}, u32[]{:S(2)}) collective-permute-start(bf16[64,2048]{1,0:T(8,128)(2,1)} %get-tuple-element.29), channel_id=1, source_target_pairs={{0,1},{4,5},{8,9},{12,13},{16,17},{20,21},{24,25},{28,29}} | collective-permute-start | bytes 786440 | tf_op jit(solution)/shard_map/ppermute | solution.py:58
  25.3 10.9 %collective-permute-start.9 = (bf16[64,2048]{1,0:T(8,128)(2,1)}, bf16[64,2048]{1,0:T(8,128)(2,1)}, u32[]{:S(2)}, u32[]{:S(2)}) collective-permute-start(bf16[64,2048]{1,0:T(8,128)(2,1)} %get-tuple-element.30), channel_id=1, source_target_pairs={{3,2},{7,6},{11,10},{15,14},{19,18},{23,22},{27,26},{31,30}} | collective-permute-start | bytes 786440 | tf_op jit(solution)/shard_map/ppermute | solution.py:59
  29.3 12.7 %copy-start.2 = (bf16[256,2048]{1,0:T(8,128)(2,1)S(1)}, bf16[256,2048]{1,0:T(8,128)(2,1)}, u32[]{:S(2)}) copy-start(bf16[256,2048]{1,0:T(8,128)(2,1)} %copy-done.1) | copy-start | bytes 3145732
  29.3 35.4 %collective-permute-start.19 = (f32[5,1024]{1,0:T(8,128)S(1)}, f32[5,1024]{1,0:T(8,128)S(1)}, u32[]{:S(2)}, u32[]{:S(2)}) collective-permute-start(f32[5,1024]{1,0:T(8,128)S(1)} %stack.23), channel_id=1, source_target_pairs={{0,4},{4,0},{8,12},{12,8},{16,20},{20,16},{24,28},{28,24},{1,5},{5... | collective-permute-start | bytes 61448 | tf_op jit(solution)/shard_map/ppermute | solution.py:34
  31.0 10.9 %collective-permute-start.4 = (bf16[64,2048]{1,0:T(8,128)(2,1)S(1)}, bf16[64,2048]{1,0:T(8,128)(2,1)S(1)}, u32[]{:S(2)}, u32[]{:S(2)}) collective-permute-start(bf16[64,2048]{1,0:T(8,128)(2,1)S(1)} %get-tuple-element.25), channel_id=1, source_target_pairs={{0,1},{1,2},{4,5},{5,6},{8,9},{9,10},{12,13},{13,14},{16,17},{17,1... | collective-permute-start | bytes 786440 | tf_op jit(solution)/shard_map/ppermute | solution.py:58
  35.4 6.5 %collective-permute-start.5 = (bf16[64,2048]{1,0:T(8,128)(2,1)S(1)}, bf16[64,2048]{1,0:T(8,128)(2,1)S(1)}, u32[]{:S(2)}, u32[]{:S(2)}) collective-permute-start(bf16[64,2048]{1,0:T(8,128)(2,1)S(1)} %get-tuple-element.26), channel_id=1, source_target_pairs={{3,2},{2,1},{7,6},{6,5},{11,10},{10,9},{15,14},{14,13},{19,18},{18... | collective-permute-start | bytes 786440 | tf_op jit(solution)/shard_map/ppermute | solution.py:59
  37.5 12.7 %collective-permute-start.10 = (bf16[64,2048]{1,0:T(8,128)(2,1)S(1)}, bf16[64,2048]{1,0:T(8,128)(2,1)S(1)}, u32[]{:S(2)}, u32[]{:S(2)}) collective-permute-start(bf16[64,2048]{1,0:T(8,128)(2,1)S(1)} %get-tuple-element.31), channel_id=1, source_target_pairs={{0,1},{1,2},{4,5},{5,6},{8,9},{9,10},{12,13},{13,14},{16,17},{17,1... | collective-permute-start | bytes 786440 | tf_op jit(solution)/shard_map/ppermute | solution.py:58
  41.2 9.0 %collective-permute-start.11 = (bf16[64,2048]{1,0:T(8,128)(2,1)S(1)}, bf16[64,2048]{1,0:T(8,128)(2,1)S(1)}, u32[]{:S(2)}, u32[]{:S(2)}) collective-permute-start(bf16[64,2048]{1,0:T(8,128)(2,1)S(1)} %get-tuple-element.32), channel_id=1, source_target_pairs={{3,2},{2,1},{7,6},{6,5},{11,10},{10,9},{15,14},{14,13},{19,18},{18... | collective-permute-start | bytes 786440 | tf_op jit(solution)/shard_map/ppermute | solution.py:59
  42.1 22.1 %copy-start.4 = (f32[4096]{0:T(1024)S(1)}, f32[4096]{0:T(1024)}, u32[]{:S(2)}) copy-start(f32[4096]{0:T(1024)} %param.8) | copy-start | bytes 49156
  42.1 14.9 %collective-permute-start.6 = (bf16[64,2048]{1,0:T(8,128)(2,1)S(1)}, bf16[64,2048]{1,0:T(8,128)(2,1)S(1)}, u32[]{:S(2)}, u32[]{:S(2)}) collective-permute-start(bf16[64,2048]{1,0:T(8,128)(2,1)S(1)} %get-tuple-element.27), channel_id=1, source_target_pairs={{0,1},{1,2},{2,3},{4,5},{5,6},{6,7},{8,9},{9,10},{10,11},{12,13},{... | collective-permute-start | bytes 786440 | tf_op jit(solution)/shard_map/ppermute | solution.py:58
  48.9 9.1 %collective-permute-start.7 = (bf16[64,2048]{1,0:T(8,128)(2,1)S(1)}, bf16[64,2048]{1,0:T(8,128)(2,1)S(1)}, u32[]{:S(2)}, u32[]{:S(2)}) collective-permute-start(bf16[64,2048]{1,0:T(8,128)(2,1)S(1)} %get-tuple-element.28), channel_id=1, source_target_pairs={{3,2},{2,1},{1,0},{7,6},{6,5},{5,4},{11,10},{10,9},{9,8},{15,14},{... | collective-permute-start | bytes 786440 | tf_op jit(solution)/shard_map/ppermute | solution.py:59
  50.4 9.6 %collective-permute-start.12 = (bf16[64,2048]{1,0:T(8,128)(2,1)S(1)}, bf16[64,2048]{1,0:T(8,128)(2,1)S(1)}, u32[]{:S(2)}, u32[]{:S(2)}) collective-permute-start(bf16[64,2048]{1,0:T(8,128)(2,1)S(1)} %get-tuple-element.33), channel_id=1, source_target_pairs={{0,1},{1,2},{2,3},{4,5},{5,6},{6,7},{8,9},{9,10},{10,11},{12,13},{... | collective-permute-start | bytes 786440 | tf_op jit(solution)/shard_map/ppermute | solution.py:58
  55.7 8.4 %collective-permute-start.13 = (bf16[64,2048]{1,0:T(8,128)(2,1)S(1)}, bf16[64,2048]{1,0:T(8,128)(2,1)S(1)}, u32[]{:S(2)}, u32[]{:S(2)}) collective-permute-start(bf16[64,2048]{1,0:T(8,128)(2,1)S(1)} %get-tuple-element.34), channel_id=1, source_target_pairs={{3,2},{2,1},{1,0},{7,6},{6,5},{5,4},{11,10},{10,9},{9,8},{15,14},{... | collective-permute-start | bytes 786440 | tf_op jit(solution)/shard_map/ppermute | solution.py:59
  64.7 2.0 %collective-permute-start.14 = (f32[4096]{0:T(1024)S(1)}, f32[4096]{0:T(1024)S(1)}, u32[]{:S(2)}, u32[]{:S(2)}) collective-permute-start(f32[4096]{0:T(1024)S(1)} %get-tuple-element.44), channel_id=1, source_target_pairs={{0,4},{4,0},{8,12},{12,8},{16,20},{20,16},{24,28},{28,24},{1,5},{5... | collective-permute-start | bytes 49160 | tf_op jit(solution)/shard_map/ppermute | solution.py:34
  64.8 4.0 %collective-permute-start.20 = (f32[5,1024]{1,0:T(8,128)S(1)}, f32[5,1024]{1,0:T(8,128)S(1)}, u32[]{:S(2)}, u32[]{:S(2)}) collective-permute-start(f32[5,1024]{1,0:T(8,128)S(1)} %add.227), channel_id=1, source_target_pairs={{0,8},{4,12},{8,0},{12,4},{16,24},{20,28},{24,16},{28,20},{1,9},{5... | collective-permute-start | bytes 61448 | tf_op jit(solution)/shard_map/ppermute | solution.py:34
  66.7 5.8 %collective-permute-start.15 = (f32[4096]{0:T(1024)S(1)}, f32[4096]{0:T(1024)S(1)}, u32[]{:S(2)}, u32[]{:S(2)}) collective-permute-start(f32[4096]{0:T(1024)S(1)} %add.222), channel_id=1, source_target_pairs={{0,8},{4,12},{8,0},{12,4},{16,24},{20,28},{24,16},{28,20},{1,9},{5... | collective-permute-start | bytes 49160 | tf_op jit(solution)/shard_map/ppermute | solution.py:34
  68.8 5.8 %collective-permute-start.21 = (f32[5,1024]{1,0:T(8,128)S(1)}, f32[5,1024]{1,0:T(8,128)S(1)}, u32[]{:S(2)}, u32[]{:S(2)}) collective-permute-start(f32[5,1024]{1,0:T(8,128)S(1)} %add.228), channel_id=1, source_target_pairs={{0,16},{4,20},{8,24},{12,28},{16,0},{20,4},{24,8},{28,12},{1,17},{... | collective-permute-start | bytes 61448 | tf_op jit(solution)/shard_map/ppermute | solution.py:34
  72.5 3.8 %collective-permute-start.16 = (f32[4096]{0:T(1024)S(1)}, f32[4096]{0:T(1024)S(1)}, u32[]{:S(2)}, u32[]{:S(2)}) collective-permute-start(f32[4096]{0:T(1024)S(1)} %add.223), channel_id=1, source_target_pairs={{0,16},{4,20},{8,24},{12,28},{16,0},{20,4},{24,8},{28,12},{1,17},{... | collective-permute-start | bytes 49160 | tf_op jit(solution)/shard_map/ppermute | solution.py:34
  76.3 3.7 %collective-permute-start.17 = (f32[4096]{0:T(1024)S(1)}, f32[4096]{0:T(1024)S(1)}, u32[]{:S(2)}, u32[]{:S(2)}) collective-permute-start(f32[4096]{0:T(1024)S(1)} %add.224), channel_id=1, source_target_pairs={{0,1},{1,0},{2,3},{3,2},{4,5},{5,4},{6,7},{7,6},{8,9},{9,8},{10,11... | collective-permute-start | bytes 49160 | tf_op jit(solution)/shard_map/ppermute | solution.py:34
  80.0 4.6 %collective-permute-start.18 = (f32[4096]{0:T(1024)S(1)}, f32[4096]{0:T(1024)S(1)}, u32[]{:S(2)}, u32[]{:S(2)}) collective-permute-start(f32[4096]{0:T(1024)S(1)} %add.225), channel_id=1, source_target_pairs={{0,2},{1,3},{2,0},{3,1},{4,6},{5,7},{6,4},{7,5},{8,10},{9,11},{10,... | collective-permute-start | bytes 49160 | tf_op jit(solution)/shard_map/ppermute | solution.py:34
  (6 other events, 28.7 us)
